TPU v7x, 8 devices: a whole 2x2x1 slice. The times are simulated.
8 devices in a mesh: dp: 1 (over z), cy: 2 (over y), cx: 4 (over x, core).
Axes of the slice: x: 2, y: 2, z: 1, core: 2. Of those that a mesh axis runs over, the one named last changes fastest.
Arguments:
- q: bfloat16 [1024, 28, 128], P(('dp', 'cy', 'cx'))
- k: bfloat16 [1024, 4, 128], P(('dp', 'cy', 'cx'))
- v: bfloat16 [1024, 4, 128], P(('dp', 'cy', 'cx'))
Outputs:
- output: bfloat16 [1024, 28, 128], P(('dp', 'cy', 'cx'))
All inputs are finite; a program needn't handle non-finite values.
Results may differ from a plain program's by a relative error of at most 0.00334014.
Values are sent between devices in bfloat16 or wider.
A program may use at most 1 GiB of HBM per device.

v0:
```python
import jax
import jax.numpy as jnp
from jax import lax
from jax.sharding import PartitionSpec as P

NEG = -1.0e30


def init_state(c, value_a3, rep, hd):
    return (jnp.full((value_a3, rep, c), NEG, jnp.float32),
            jnp.zeros((value_a3, rep, c), jnp.float32),
            jnp.zeros((value_a3, rep, c, hd), jnp.float32))


def update(state, qc, kc, vc, mask, scale):
    m, l, acc = state
    s = jnp.einsum('qgrd,kgd->grqk', qc, kc, preferred_element_type=jnp.float32) * scale
    if mask is not None:
        s = jnp.where(mask, s, NEG)
    mn = jnp.maximum(m, jnp.max(s, axis=-1))
    p = jnp.exp(s - mn[..., None])
    alpha = jnp.exp(m - mn)
    l = alpha * l + jnp.sum(p, axis=-1)
    pv = jnp.einsum('grqk,kgd->grqd', p.astype(jnp.bfloat16), vc, preferred_element_type=jnp.float32)
    return (mn, l, alpha[..., None] * acc + pv)


def finish(state, c, nh, hd):
    m, l, acc = state
    o = (acc / l[..., None]).astype(jnp.bfloat16)
    return o.transpose(2, 0, 1, 3).reshape(c, nh, hd)


def solution(mesh):
    ncx = mesh.shape['cx']
    n = mesh.shape['cy'] * ncx
    axes = ('cy', 'cx')
    perm = [(i, (i + 1) % n) for i in range(n)]
    spec = P(('dp', 'cy', 'cx'))

    def local(q, k, v):
        t, nh, hd = q.shape
        value_a3 = k.shape[1]
        rep = nh // value_a3
        c = t // 2
        scale = hd ** -0.5
        r = lax.axis_index('cy') * ncx + lax.axis_index('cx')
        qa = q[:c].reshape(c, value_a3, rep, hd)
        qb = q[c:].reshape(c, value_a3, rep, hd)
        tri = jnp.arange(c)[None, :] <= jnp.arange(c)[:, None]
        sa = update(init_state(c, value_a3, rep, hd), qa, k[:c], v[:c], tri, scale)
        sb = update(init_state(c, value_a3, rep, hd), qb, k[:c], v[:c], None, scale)
        sb = update(sb, qb, k[c:], v[c:], tri, scale)
        kb = k
        vb = v
        for hop in range(1, n):
            kb = lax.ppermute(kb, axes, perm)
            vb = lax.ppermute(vb, axes, perm)
            src = (r - hop) % n
            sb = update(sb, qb, kb[:c], vb[:c], None, scale)
            lower = src < r
            qx = jnp.where(lower, qa, qb)
            kx = jnp.where(lower, kb[:c], kb[c:])
            vx = jnp.where(lower, vb[:c], vb[c:])
            sx = tuple(jnp.where(lower, a, b) for a, b in zip(sa, sb))
            sx = update(sx, qx, kx, vx, None, scale)
            sa = tuple(jnp.where(lower, a, b) for a, b in zip(sx, sa))
            sb = tuple(jnp.where(lower, b, a) for a, b in zip(sx, sb))
        return jnp.concatenate([finish(sa, c, nh, hd), finish(sb, c, nh, hd)], axis=0)

    return jax.shard_map(local, mesh=mesh, in_specs=(spec, spec, spec), out_specs=spec, check_vma=False)
```

profile of v0, /device:TPU:0, one launch (start us, length us, event | category | flops | bytes accessed | tf_op | source)
XLA Modules:
  0.0 58.3 jit_solution(8756462540476383243)
XLA Ops:
  0.0 0.9 %copy.4 = bf16[128,4,128]{2,0,1:T(8,128)(2,1)S(1)} copy(bf16[128,4,128]{2,1,0:T(4,128)(2,1)} %param.4) | data formatting | bytes 262144 | tf_op args[1]
  0.9 0.9 %collective-permute-start = (bf16[128,4,128]{2,0,1:T(8,128)(2,1)S(1)}, bf16[128,4,128]{2,0,1:T(8,128)(2,1)S(1)}, u32[]{:S(2)}, u32[]{:S(2)}) collective-permute-start(bf16[128,4,128]{2,0,1:T(8,128)(2,1)S(1)} %copy.4), channel_id=1, source_target_pairs={{0,1},{1,2},{2,3},{3,4},{4,5},{5,6},{6,7},{7,0}} | collective-permute-start | bytes 393224 | tf_op jit(solution)/shard_map/ppermute | solution.py:57
  1.8 0.9 %copy.7 = bf16[128,4,128]{2,0,1:T(8,128)(2,1)S(1)} copy(bf16[128,4,128]{2,1,0:T(4,128)(2,1)} %param.5) | data formatting | bytes 262144 | tf_op args[2]
  2.7 2.6 %collective-permute-start.7 = (bf16[128,4,128]{2,0,1:T(8,128)(2,1)S(1)}, bf16[128,4,128]{2,0,1:T(8,128)(2,1)S(1)}, u32[]{:S(2)}, u32[]{:S(2)}) collective-permute-start(bf16[128,4,128]{2,0,1:T(8,128)(2,1)S(1)} %copy.7), channel_id=1, source_target_pairs={{0,1},{1,2},{2,3},{3,4},{4,5},{5,6},{6,7},{7,0}} | collective-permute-start | bytes 393224 | tf_op jit(solution)/shard_map/ppermute | solution.py:58
  5.5 1.2 %fusion.217 = (bf16[64,28,128]{2,0,1:T(8,128)(2,1)S(1)}, bf16[64,28,128]{2,0,1:T(8,128)(2,1)S(1)}) fusion(bf16[128,28,128]{2,0,1:T(8,128)(2,1)} %param.3), kind=kLoop, calls=%fused_computation.354 | loop fusion | bytes 1835008 | tf_op jit(solution)/shard_map/slice | solution.py:48
  6.7 0.5 fusion.223
  7.3 0.5 fusion.218
  7.8 0.5 fusion.224
  8.4 0.5 fusion.221
  9.0 1.6 %collective-permute-start.8 = (bf16[128,4,128]{2,0,1:T(8,128)(2,1)S(1)}, bf16[128,4,128]{2,0,1:T(8,128)(2,1)S(1)}, u32[]{:S(2)}, u32[]{:S(2)}) collective-permute-start(bf16[128,4,128]{2,0,1:T(8,128)(2,1)S(1)} %collective-permute-done.7), channel_id=1, source_target_pairs={{0,1},{1,2},{2,3},{3,4},{4,5},{5,6},{6,7},{7,0}} | collective-permute-start | bytes 393224 | tf_op jit(solution)/shard_map/ppermute | solution.py:58
  10.6 0.5 fusion.222
  11.1 2.6 %collective-permute-done.1 = bf16[128,4,128]{2,0,1:T(8,128)(2,1)S(1)} collective-permute-done((bf16[128,4,128]{2,0,1:T(8,128)(2,1)S(1)}, bf16[128,4,128]{2,0,1:T(8,128)(2,1)S(1)}, u32[]{:S(2)}, u32[]{:S(2)}) %collective-permute-start.1) | collective-permute-done | bytes 131104 | tf_op jit(solution)/shard_map/ppermute | solution.py:57
  13.7 0.5 fusion.220
  14.2 0.5 fusion.219
  14.8 0.3 convolution_bitcast_fusion.14
  15.1 0.5 fusion.34
  15.6 0.5 fusion.38
  16.0 0.4 fusion.32
  16.5 1.5 %fusion.4 = f32[64,4,7,128]{3,0,2,1:T(8,128)S(1)} fusion(f32[64,4,7,128]{3,0,2,1:T(8,128)S(1)} %convolution_bitcast_fusion.14, f32[4,7,64,64]{2,3,1,0:T(8,128)S(1)} %get-tuple-element.84, f32[4,7,64]{2,1,0:T(8,128)S(1)} %get-tuple-element.70, f32[64,4,7]{0,2,1:T(8,128)S(1)} %get-tuple-element.68, f32[64,4,7]{0,2,1:T(8,128)S(1)} %get-tuple-element.66, ...), kind=kOutput, calls=%fused_computation.21 | convolution fusion | flops 30507008 | bytes 2883584 | tf_op jit(solution)/shard_map/grqk,kgd->grqd/dot_general | solution.py:24
  18.1 0.3 fusion.5
  18.4 0.7 %collective-permute-start.9 = (bf16[128,4,128]{2,0,1:T(8,128)(2,1)S(1)}, bf16[128,4,128]{2,0,1:T(8,128)(2,1)S(1)}, u32[]{:S(2)}, u32[]{:S(2)}) collective-permute-start(bf16[128,4,128]{2,0,1:T(8,128)(2,1)S(1)} %collective-permute-done.8), channel_id=1, source_target_pairs={{0,1},{1,2},{2,3},{3,4},{4,5},{5,6},{6,7},{7,0}} | collective-permute-start | bytes 393224 | tf_op jit(solution)/shard_map/ppermute | solution.py:58
  19.1 0.3 convolution_bitcast_fusion.10
  19.5 0.2 fusion.44
  19.7 3.7 %collective-permute-done.2 = bf16[128,4,128]{2,0,1:T(8,128)(2,1)S(1)} collective-permute-done((bf16[128,4,128]{2,0,1:T(8,128)(2,1)S(1)}, bf16[128,4,128]{2,0,1:T(8,128)(2,1)S(1)}, u32[]{:S(2)}, u32[]{:S(2)}) %collective-permute-start.2) | collective-permute-done | bytes 131104 | tf_op jit(solution)/shard_map/ppermute | solution.py:57
  23.3 0.5 fusion.227
  23.9 0.9 %collective-permute-done.9 = bf16[128,4,128]{2,0,1:T(8,128)(2,1)S(1)} collective-permute-done((bf16[128,4,128]{2,0,1:T(8,128)(2,1)S(1)}, bf16[128,4,128]{2,0,1:T(8,128)(2,1)S(1)}, u32[]{:S(2)}, u32[]{:S(2)}) %collective-permute-start.9) | collective-permute-done | bytes 131104 | tf_op jit(solution)/shard_map/ppermute | solution.py:58
  24.7 0.5 fusion.228
  25.3 3.4 %collective-permute-done.3 = bf16[128,4,128]{2,0,1:T(8,128)(2,1)S(1)} collective-permute-done((bf16[128,4,128]{2,0,1:T(8,128)(2,1)S(1)}, bf16[128,4,128]{2,0,1:T(8,128)(2,1)S(1)}, u32[]{:S(2)}, u32[]{:S(2)}) %collective-permute-start.3) | collective-permute-done | bytes 131104 | tf_op jit(solution)/shard_map/ppermute | solution.py:57
  28.6 0.5 fusion.226
  29.2 0.5 fusion.225
  29.7 0.5 fusion.46
  30.2 0.5 fusion.48
  30.6 0.1 bitcast_add_fusion.7
  30.7 0.5 fusion
  31.2 0.7 %fusion.6 = f32[64,4,7,128]{3,0,2,1:T(8,128)S(1)} fusion(f32[64,4,7,128]{3,0,2,1:T(8,128)S(1)} %fusion, f32[64,4,7,128]{3,0,2,1:T(8,128)S(1)} %fusion.5, f32[4,7,64,64]{2,3,1,0:T(8,128)S(1)} %get-tuple-element.78, f32[4,7,64]{2,1,0:T(8,128)S(1)} %get-tuple-element.61, f32[64,4,7]{0,2,1:T(8,128)S(1)} %get-tuple-element.40, pred[]{:T(512)S(6)} %lt.64, ...), kind=kOutput, calls=%fused_computation.23 | convolution fusion | flops 30310400 | bytes 3357696 | tf_op jit(solution)/shard_map/grqk,kgd->grqd/dot_general | solution.py:24
  31.9 0.5 fusion.7
  32.4 1.1 %fusion.8 = f32[64,4,7,128]{3,0,2,1:T(8,128)S(1)} fusion(f32[64,4,7,128]{3,0,2,1:T(8,128)S(1)} %fusion.7, f32[64,4,7,128]{3,0,2,1:T(8,128)S(1)} %convolution_bitcast_fusion.10, f32[4,7,64,64]{2,3,1,0:T(8,128)S(1)} %get-tuple-element.92, f32[4,7,64]{2,1,0:T(8,128)S(1)} %get-tuple-element.55, f32[64,4,7]{0,2,1:T(8,128)S(1)} %get-tuple-element.34, ...), kind=kOutput, calls=%fused_computation.25 | convolution fusion | flops 31195136 | bytes 5619714 | tf_op jit(solution)/shard_map/grqk,kgd->grqd/dot_general | solution.py:24
  33.5 1.1 %fusion.67 = (f32[64,4,7,128]{3,0,2,1:T(8,128)S(1)}, f32[64,4,7,128]{3,0,2,1:T(8,128)S(1)}, f32[64,4,7,128]{3,0,2,1:T(8,128)S(1)}) fusion(f32[64,4,7,128]{3,0,2,1:T(8,128)S(1)} %fusion.8, f32[64,4,7]{0,2,1:T(8,128)S(1)} %get-tuple-element.29, pred[]{:T(512)S(6)} %lt.60, f32[64,4,7,128]{3,0,2,1:T(8,128)S(1)} %convolution_bitcast_fusion.10, ...), kind=kOutput, calls=%fused_computation.127 | convolution fusion | flops 31686656 | bytes 7953408 | tf_op jit(solution)/shard_map/grqk,kgd->grqd/dot_general | solution.py:24
  34.6 1.1 %fusion.9 = f32[64,4,7,128]{3,0,2,1:T(8,128)S(1)} fusion(f32[64,4,7,128]{3,0,2,1:T(8,128)S(1)} %fusion.8, f32[64,4,7,128]{3,0,2,1:T(8,128)S(1)} %get-tuple-element.93, f32[64,4,7,128]{3,0,2,1:T(8,128)S(1)} %get-tuple-element.57, f32[4,7,64,64]{2,3,1,0:T(8,128)S(1)} %get-tuple-element.88, f32[4,7,64]{2,1,0:T(8,128)S(1)} %get-tuple-element.53, ...), kind=kOutput, calls=%fused_computation.26 | convolution fusion | flops 30965760 | bytes 4702209 | tf_op jit(solution)/shard_map/grqk,kgd->grqd/dot_general | solution.py:24
  35.7 0.3 convolution_bitcast_fusion.6
  36.1 0.4 collective-permute-done.4
  36.5 0.5 fusion.233
  37.0 4.4 %collective-permute-done.11 = bf16[128,4,128]{2,0,1:T(8,128)(2,1)S(1)} collective-permute-done((bf16[128,4,128]{2,0,1:T(8,128)(2,1)S(1)}, bf16[128,4,128]{2,0,1:T(8,128)(2,1)S(1)}, u32[]{:S(2)}, u32[]{:S(2)}) %collective-permute-start.11) | collective-permute-done | bytes 131104 | tf_op jit(solution)/shard_map/ppermute | solution.py:58
  41.4 0.5 fusion.234
  41.9 0.9 %collective-permute-done.5 = bf16[128,4,128]{2,0,1:T(8,128)(2,1)S(1)} collective-permute-done((bf16[128,4,128]{2,0,1:T(8,128)(2,1)S(1)}, bf16[128,4,128]{2,0,1:T(8,128)(2,1)S(1)}, u32[]{:S(2)}, u32[]{:S(2)}) %collective-permute-start.5) | collective-permute-done | bytes 131104 | tf_op jit(solution)/shard_map/ppermute | solution.py:57
  42.8 0.5 fusion.231
  43.3 3.4 %collective-permute-done.12 = bf16[128,4,128]{2,0,1:T(8,128)(2,1)S(1)} collective-permute-done((bf16[128,4,128]{2,0,1:T(8,128)(2,1)S(1)}, bf16[128,4,128]{2,0,1:T(8,128)(2,1)S(1)}, u32[]{:S(2)}, u32[]{:S(2)}) %collective-permute-start.12) | collective-permute-done | bytes 131104 | tf_op jit(solution)/shard_map/ppermute | solution.py:58
  46.7 0.5 fusion.232
  47.2 0.9 %collective-permute-done.6 = bf16[128,4,128]{2,0,1:T(8,128)(2,1)S(1)} collective-permute-done((bf16[128,4,128]{2,0,1:T(8,128)(2,1)S(1)}, bf16[128,4,128]{2,0,1:T(8,128)(2,1)S(1)}, u32[]{:S(2)}, u32[]{:S(2)}) %collective-permute-start.6) | collective-permute-done | bytes 131104 | tf_op jit(solution)/shard_map/ppermute | solution.py:57
  48.1 0.5 fusion.230
  48.6 0.5 fusion.229
  49.2 0.2 fusion.64
  49.4 0.2 fusion.62
  49.6 0.5 fusion.58
  50.0 0.5 fusion.54
  50.5 0.1 bitcast_add_fusion.3
  50.6 0.3 convolution_bitcast_fusion.2
  51.0 1.1 %fusion.10 = f32[64,4,7,128]{3,0,2,1:T(8,128)S(1)} fusion(f32[64,4,7,128]{3,0,2,1:T(8,128)S(1)} %fusion.9, f32[64,4,7,128]{3,0,2,1:T(8,128)S(1)} %convolution_bitcast_fusion.6, f32[64,4,7,128]{3,0,2,1:T(8,128)S(1)} %get-tuple-element.56, f32[4,7,64,64]{2,3,1,0:T(8,128)S(1)} %get-tuple-element.105, f32[4,7,64]{2,1,0:T(8,128)S(1)} %get-tuple-element.48, ...), kind=kOutput, calls=%fused_computation.27 | convolution fusion | flops 30965760 | bytes 4702209 | tf_op jit(solution)/shard_map/grqk,kgd->grqd/dot_general | solution.py:24
  52.1 1.1 %fusion.69 = (f32[64,4,7,128]{3,0,2,1:T(8,128)S(1)}, f32[64,4,7,128]{3,0,2,1:T(8,128)S(1)}, f32[64,4,7,128]{3,0,2,1:T(8,128)S(1)}) fusion(f32[64,4,7,128]{3,0,2,1:T(8,128)S(1)} %fusion.10, f32[64,4,7]{0,2,1:T(8,128)S(1)} %get-tuple-element.18, pred[]{:T(512)S(6)} %lt.56, f32[64,4,7,128]{3,0,2,1:T(8,128)S(1)} %get-tuple-element.56, ...), kind=kOutput, calls=%fused_computation.129 | convolution fusion | flops 31457280 | bytes 7035392 | tf_op jit(solution)/shard_map/grqk,kgd->grqd/dot_general | solution.py:24
  53.2 1.1 %fusion.11 = f32[64,4,7,128]{3,0,2,1:T(8,128)S(1)} fusion(f32[64,4,7,128]{3,0,2,1:T(8,128)S(1)} %fusion.10, f32[64,4,7,128]{3,0,2,1:T(8,128)S(1)} %get-tuple-element.106, f32[64,4,7,128]{3,0,2,1:T(8,128)S(1)} %get-tuple-element.50, f32[4,7,64,64]{2,3,1,0:T(8,128)S(1)} %get-tuple-element.101, f32[4,7,64]{2,1,0:T(8,128)S(1)} %get-tuple-element.46, ...), kind=kOutput, calls=%fused_computation.28 | convolution fusion | flops 30965760 | bytes 4702209 | tf_op jit(solution)/shard_map/grqk,kgd->grqd/dot_general | solution.py:24
  54.3 1.1 %fusion.12 = f32[64,4,7,128]{3,0,2,1:T(8,128)S(1)} fusion(f32[64,4,7,128]{3,0,2,1:T(8,128)S(1)} %fusion.11, f32[64,4,7,128]{3,0,2,1:T(8,128)S(1)} %convolution_bitcast_fusion.2, f32[64,4,7,128]{3,0,2,1:T(8,128)S(1)} %get-tuple-element.49, f32[4,7,64,64]{2,3,1,0:T(8,128)S(1)} %get-tuple-element.97, f32[4,7,64]{2,1,0:T(8,128)S(1)} %get-tuple-element.44, ...), kind=kOutput, calls=%fused_computation.29 | convolution fusion | flops 30965760 | bytes 4702209 | tf_op jit(solution)/shard_map/grqk,kgd->grqd/dot_general | solution.py:24
  55.4 1.3 %divide_convert_fusion.1 = (bf16[64,4,7,128]{3,0,2,1:T(8,128)(2,1)S(1)}, f32[64,4,7,128]{3,0,2,1:T(8,128)S(1)}, f32[64,4,7,128]{3,0,2,1:T(8,128)S(1)}) fusion(f32[64,4,7,128]{3,0,2,1:T(8,128)S(1)} %fusion.12, f32[64,4,7]{0,2,1:T(8,128)S(1)} %get-tuple-element.7, f32[64,4,7]{0,2,1:T(8,128)S(1)} %get-tuple-element.8, pred[]{:T(512)S(6)} %lt.52, ...), kind=kOutput, calls=%fused_computation.68 | convolution fusion | flops 31916032 | bytes 6583808 | tf_op jit(solution)/shard_map/grqk,kgd->grqd/dot_general | solution.py:24
  56.8 0.6 divide_convert_fusion
  57.3 1.0 %pad_maximum_fusion = bf16[128,28,128]{2,0,1:T(8,128)(2,1)} fusion(bf16[64,28,128]{2,0,1:T(8,128)(2,1)S(1)} %bitcast.615, bf16[64,28,128]{2,0,1:T(8,128)(2,1)S(1)} %bitcast.614), kind=kLoop, calls=%fused_computation.66 | loop fusion | flops 1835008 | bytes 1835008 | tf_op jit(solution)/shard_map/concatenate | solution.py:69
  (22 shorter events, 0.3 us)
Async XLA Ops:
  0.9 7.4 %collective-permute-start = (bf16[128,4,128]{2,0,1:T(8,128)(2,1)S(1)}, bf16[128,4,128]{2,0,1:T(8,128)(2,1)S(1)}, u32[]{:S(2)}, u32[]{:S(2)}) collective-permute-start(bf16[128,4,128]{2,0,1:T(8,128)(2,1)S(1)} %copy.4), channel_id=1, source_target_pairs={{0,1},{1,2},{2,3},{3,4},{4,5},{5,6},{6,7},{7,0}} | collective-permute-start | bytes 393224 | tf_op jit(solution)/shard_map/ppermute | solution.py:57
  2.7 6.2 %collective-permute-start.7 = (bf16[128,4,128]{2,0,1:T(8,128)(2,1)S(1)}, bf16[128,4,128]{2,0,1:T(8,128)(2,1)S(1)}, u32[]{:S(2)}, u32[]{:S(2)}) collective-permute-start(bf16[128,4,128]{2,0,1:T(8,128)(2,1)S(1)} %copy.7), channel_id=1, source_target_pairs={{0,1},{1,2},{2,3},{3,4},{4,5},{5,6},{6,7},{7,0}} | collective-permute-start | bytes 393224 | tf_op jit(solution)/shard_map/ppermute | solution.py:58
  8.4 5.3 %collective-permute-start.1 = (bf16[128,4,128]{2,0,1:T(8,128)(2,1)S(1)}, bf16[128,4,128]{2,0,1:T(8,128)(2,1)S(1)}, u32[]{:S(2)}, u32[]{:S(2)}) collective-permute-start(bf16[128,4,128]{2,0,1:T(8,128)(2,1)S(1)} %collective-permute-done), channel_id=1, source_target_pairs={{0,1},{1,2},{2,3},{3,4},{4,5},{5,6},{6,7},{7,0}} | collective-permute-start | bytes 393224 | tf_op jit(solution)/shard_map/ppermute | solution.py:57
  9.0 9.5 %collective-permute-start.8 = (bf16[128,4,128]{2,0,1:T(8,128)(2,1)S(1)}, bf16[128,4,128]{2,0,1:T(8,128)(2,1)S(1)}, u32[]{:S(2)}, u32[]{:S(2)}) collective-permute-start(bf16[128,4,128]{2,0,1:T(8,128)(2,1)S(1)} %collective-permute-done.7), channel_id=1, source_target_pairs={{0,1},{1,2},{2,3},{3,4},{4,5},{5,6},{6,7},{7,0}} | collective-permute-start | bytes 393224 | tf_op jit(solution)/shard_map/ppermute | solution.py:58
  18.0 5.3 %collective-permute-start.2 = (bf16[128,4,128]{2,0,1:T(8,128)(2,1)S(1)}, bf16[128,4,128]{2,0,1:T(8,128)(2,1)S(1)}, u32[]{:S(2)}, u32[]{:S(2)}) collective-permute-start(bf16[128,4,128]{2,0,1:T(8,128)(2,1)S(1)} %collective-permute-done.1), channel_id=1, source_target_pairs={{0,1},{1,2},{2,3},{3,4},{4,5},{5,6},{6,7},{7,0}} | collective-permute-start | bytes 393224 | tf_op jit(solution)/shard_map/ppermute | solution.py:57
  18.4 6.3 %collective-permute-start.9 = (bf16[128,4,128]{2,0,1:T(8,128)(2,1)S(1)}, bf16[128,4,128]{2,0,1:T(8,128)(2,1)S(1)}, u32[]{:S(2)}, u32[]{:S(2)}) collective-permute-start(bf16[128,4,128]{2,0,1:T(8,128)(2,1)S(1)} %collective-permute-done.8), channel_id=1, source_target_pairs={{0,1},{1,2},{2,3},{3,4},{4,5},{5,6},{6,7},{7,0}} | collective-permute-start | bytes 393224 | tf_op jit(solution)/shard_map/ppermute | solution.py:58
  23.3 5.3 %collective-permute-start.3 = (bf16[128,4,128]{2,0,1:T(8,128)(2,1)S(1)}, bf16[128,4,128]{2,0,1:T(8,128)(2,1)S(1)}, u32[]{:S(2)}, u32[]{:S(2)}) collective-permute-start(bf16[128,4,128]{2,0,1:T(8,128)(2,1)S(1)} %collective-permute-done.2), channel_id=1, source_target_pairs={{0,1},{1,2},{2,3},{3,4},{4,5},{5,6},{6,7},{7,0}} | collective-permute-start | bytes 393224 | tf_op jit(solution)/shard_map/ppermute | solution.py:57
  24.7 9.9 %collective-permute-start.10 = (bf16[128,4,128]{2,0,1:T(8,128)(2,1)S(1)}, bf16[128,4,128]{2,0,1:T(8,128)(2,1)S(1)}, u32[]{:S(2)}, u32[]{:S(2)}) collective-permute-start(bf16[128,4,128]{2,0,1:T(8,128)(2,1)S(1)} %collective-permute-done.9), channel_id=1, source_target_pairs={{0,1},{1,2},{2,3},{3,4},{4,5},{5,6},{6,7},{7,0}} | collective-permute-start | bytes 393224 | tf_op jit(solution)/shard_map/ppermute | solution.py:58
  31.2 5.3 %collective-permute-start.4 = (bf16[128,4,128]{2,0,1:T(8,128)(2,1)S(1)}, bf16[128,4,128]{2,0,1:T(8,128)(2,1)S(1)}, u32[]{:S(2)}, u32[]{:S(2)}) collective-permute-start(bf16[128,4,128]{2,0,1:T(8,128)(2,1)S(1)} %collective-permute-done.3), channel_id=1, source_target_pairs={{0,1},{1,2},{2,3},{3,4},{4,5},{5,6},{6,7},{7,0}} | collective-permute-start | bytes 393224 | tf_op jit(solution)/shard_map/ppermute | solution.py:57
  36.1 5.3 %collective-permute-start.11 = (bf16[128,4,128]{2,0,1:T(8,128)(2,1)S(1)}, bf16[128,4,128]{2,0,1:T(8,128)(2,1)S(1)}, u32[]{:S(2)}, u32[]{:S(2)}) collective-permute-start(bf16[128,4,128]{2,0,1:T(8,128)(2,1)S(1)} %collective-permute-done.10), channel_id=1, source_target_pairs={{0,1},{1,2},{2,3},{3,4},{4,5},{5,6},{6,7},{7,0}} | collective-permute-start | bytes 393224 | tf_op jit(solution)/shard_map/ppermute | solution.py:58
  36.5 6.3 %collective-permute-start.5 = (bf16[128,4,128]{2,0,1:T(8,128)(2,1)S(1)}, bf16[128,4,128]{2,0,1:T(8,128)(2,1)S(1)}, u32[]{:S(2)}, u32[]{:S(2)}) collective-permute-start(bf16[128,4,128]{2,0,1:T(8,128)(2,1)S(1)} %collective-permute-done.4), channel_id=1, source_target_pairs={{0,1},{1,2},{2,3},{3,4},{4,5},{5,6},{6,7},{7,0}} | collective-permute-start | bytes 393224 | tf_op jit(solution)/shard_map/ppermute | solution.py:57
  41.4 5.3 %collective-permute-start.12 = (bf16[128,4,128]{2,0,1:T(8,128)(2,1)S(1)}, bf16[128,4,128]{2,0,1:T(8,128)(2,1)S(1)}, u32[]{:S(2)}, u32[]{:S(2)}) collective-permute-start(bf16[128,4,128]{2,0,1:T(8,128)(2,1)S(1)} %collective-permute-done.11), channel_id=1, source_target_pairs={{0,1},{1,2},{2,3},{3,4},{4,5},{5,6},{6,7},{7,0}} | collective-permute-start | bytes 393224 | tf_op jit(solution)/shard_map/ppermute | solution.py:58
  42.8 5.3 %collective-permute-start.6 = (bf16[128,4,128]{2,0,1:T(8,128)(2,1)S(1)}, bf16[128,4,128]{2,0,1:T(8,128)(2,1)S(1)}, u32[]{:S(2)}, u32[]{:S(2)}) collective-permute-start(bf16[128,4,128]{2,0,1:T(8,128)(2,1)S(1)} %collective-permute-done.5), channel_id=1, source_target_pairs={{0,1},{1,2},{2,3},{3,4},{4,5},{5,6},{6,7},{7,0}} | collective-permute-start | bytes 393224 | tf_op jit(solution)/shard_map/ppermute | solution.py:57
  46.7 7.6 %collective-permute-start.13 = (bf16[128,4,128]{2,0,1:T(8,128)(2,1)S(1)}, bf16[128,4,128]{2,0,1:T(8,128)(2,1)S(1)}, u32[]{:S(2)}, u32[]{:S(2)}) collective-permute-start(bf16[128,4,128]{2,0,1:T(8,128)(2,1)S(1)} %collective-permute-done.12), channel_id=1, source_target_pairs={{0,1},{1,2},{2,3},{3,4},{4,5},{5,6},{6,7},{7,0}} | collective-permute-start | bytes 393224 | tf_op jit(solution)/shard_map/ppermute | solution.py:58
where the time goes:
time: 58.5 us; the launch traced here: 58.3 us
  matrix products  22.7 us (39%)
  waiting for transfers between devices  20.4 us (35%)
  starting transfers between devices  5.99 us (10%)
  other arithmetic  5.61 us (10%)
  local copies, waits for them, and re-layouts  3.07 us (5%)
  between operations  0.6 us (1%)
    dot_general x17, matrix products, update(): jnp.einsum('grqk,kgd->grqd', p.astype(jnp.bfloat16), vc, preferred_elemen...  13.9 us
    ppermute x7, waiting for transfers between devices, local(): kb = lax.ppermute(kb, axes, perm)  11.7 us
    dot_general x17, matrix products, update(): jnp.einsum('qgrd,kgd->grqk', qc, kc, preferred_element_type=jnp.float32)  8.81 us
    ppermute x7, waiting for transfers between devices, local(): vb = lax.ppermute(vb, axes, perm)  8.61 us
    ppermute x7, starting transfers between devices, local(): vb = lax.ppermute(vb, axes, perm)  4.99 us
    reduce_sum x10, other arithmetic, update(): l = alpha * l + jnp.sum(p, axis=-1)  3.76 us
    unnamed x2, local copies, waits for them, and re-layouts  1.85 us
    slice x1, local copies, waits for them, and re-layouts, local(): qa = q[:c].reshape(c, value_a3, rep, hd)  1.23 us
  transfers between devices with their start and end apart: 14, of which 9 were waited for; matrix products, arithmetic and copies ran while one was open for 45% of the time, Pallas kernels for 0%

commit v1 on v0

v1 whole, which is shorter than its diff:
```python
import functools
import math

import jax
import jax.numpy as jnp
from jax import lax
from jax.experimental import pallas as pl
from jax.experimental.pallas import tpu as pltpu
from jax.sharding import PartitionSpec as P

NEG = -1.0e30
MESH = pl.DeviceIdType.MESH

FIRST = (1, 2, 3, 4)
SECOND = (0, 6, 7, 5)


def kernel(q_hbm, k_hbm, v_hbm, o_hbm, qs, kin, vin, kf, g_ref, m_ref, l_ref, acc_ref, out_ref,
           in_sem, out_sem, own_send, own_recv, rel_send, rel_recv, fwd_send, fwd_recv, *, ng, rep, c, hd):
    icy = lax.axis_index('cy')
    icx = lax.axis_index('cx')
    core = icx % 2
    chip = icy * 2 + icx // 2
    xdev = {'cx': (icx + 2) % 4}
    ydev = {'cy': (icy + 1) % 2}
    sdev = {'cx': icx + 1 - 2 * core}
    chip_x = icy * 2 + (icx // 2 + 1) % 2
    chip_y = ((icy + 1) % 2) * 2 + icx // 2
    chip_d = 3 - chip

    loads = [
        pltpu.make_async_copy(k_hbm, kin, in_sem.at[0]),
        pltpu.make_async_copy(v_hbm, vin, in_sem.at[1]),
        pltpu.make_async_copy(q_hbm.at[:, 0:c, :], qs.at[0], in_sem.at[2]),
        pltpu.make_async_copy(q_hbm.at[:, c:2 * c, :], qs.at[1], in_sem.at[3]),
    ]
    for cp in loads:
        cp.start()
    barrier = pltpu.get_barrier_semaphore()
    for dev in (xdev, ydev, sdev):
        pl.semaphore_signal(barrier, inc=1, device_id=dev, device_id_type=MESH)

    for t, src in enumerate((kin, vin)):
        loads[t].wait()
        kf[t] = src[...].astype(jnp.float32)
        for g in range(ng):
            x = kf[t, pl.ds(g, 2 * c, stride=ng), :].astype(jnp.bfloat16)
            g_ref[g, FIRST[0], t, 0] = x[:c]
            g_ref[g, SECOND[0], t, 0] = x[c:]
    pl.semaphore_wait(barrier, 3)

    def remote(src, dst, send, recv, dev):
        return pltpu.make_async_remote_copy(src_ref=src, dst_ref=dst, send_sem=send, recv_sem=recv,
                                            device_id=dev, device_id_type=MESH)

    places = (FIRST, SECOND)
    own = [[[remote(g_ref.at[g, places[h][0], :, 0],
                    g_ref.at[g, places[h][(1, 2, 0)[w]], :, 0 if w < 2 else 1],
                    own_send.at[g, h, w], own_recv.at[g, h, w], (xdev, ydev, sdev)[w])
             for w in range(3)] for h in range(2)] for g in range(ng)]
    rel = [[remote(g_ref.at[g, places[h][1 + h], :, 0], g_ref.at[g, places[h][3], :, 0],
                   rel_send.at[g, h], rel_recv.at[g, h], (ydev, xdev)[h])
            for h in range(2)] for g in range(ng)]
    fwd = [[[remote(g_ref.at[g, places[h][w + 1], :, 0], g_ref.at[g, places[h][w + 1], :, 1],
                    fwd_send.at[g, h, w], fwd_recv.at[g, h, w], sdev)
             for w in range(3)] for h in range(2)] for g in range(ng)]

    for g in range(ng):
        for w in range(3):
            for h in range(2):
                own[g][h][w].start()
    for cp in loads[2:]:
        cp.wait()

    x_b = chip_x > chip
    y_b = chip_y > chip
    d_b = chip_d > chip
    mul = math.log2(math.e) * hd ** -0.5
    row = lax.broadcasted_iota(jnp.int32, (c, 2 * c), 0)
    col = lax.broadcasted_iota(jnp.int32, (c, 2 * c), 1)
    tri = col <= row
    mask_a = jnp.logical_or(tri, jnp.logical_and(col >= c, core == 1))
    mask_b = jnp.logical_or(tri, jnp.logical_and(col >= c, core == 0))

    def queries(sel, g):
        return qs[sel, rep * g:rep * (g + 1)].reshape(rep * c, hd)

    def keys(g, t, first, count):
        return g_ref[g, pl.ds(first, count), t].reshape(count * 2 * c, hd)

    def scores(q, kk):
        return lax.dot_general(q, kk, (((1,), (1,)), ((), ())), preferred_element_type=jnp.float32) * mul

    def masked(s, mask):
        n = s.shape[-1]
        return jnp.where(mask[None], s.reshape(rep, c, n), NEG).reshape(rep * c, n)

    def rowmax(s):
        return jnp.max(s, axis=-1, keepdims=True)

    def fold(p):
        return sum(p[:, i:i + 128] for i in range(0, p.shape[1], 128))

    def pv(p, g, first, count):
        return jnp.dot(p.astype(jnp.bfloat16), keys(g, 1, first, count), preferred_element_type=jnp.float32)

    tile_x = jnp.where(x_b, SECOND[1], FIRST[1])
    tile_y = jnp.where(y_b, SECOND[2], FIRST[2])
    tile_d = jnp.where(d_b, SECOND[3], FIRST[3])
    sel_x = jnp.where(x_b, 1, 0)
    sel_y = jnp.where(y_b, 1, 0)
    sel_d = jnp.where(d_b, 1, 0)

    def stage_a(g):
        qa, qb = queries(0, g), queries(1, g)
        sb = scores(qb, keys(g, 0, 0, 4))
        sb = jnp.concatenate([masked(sb[:, :2 * c], mask_b), sb[:, 2 * c:]], axis=1)
        sa = masked(scores(qa, keys(g, 0, FIRST[0], 1)), mask_a)
        sx = scores(queries(sel_x, g), keys(g, 0, tile_x, 1))
        sy = scores(queries(sel_y, g), keys(g, 0, tile_y, 1))
        mx, my = rowmax(sx), rowmax(sy)
        ma = jnp.maximum(rowmax(sa), jnp.maximum(jnp.where(x_b, NEG, mx), jnp.where(y_b, NEG, my)))
        mb = jnp.maximum(rowmax(sb), jnp.maximum(jnp.where(x_b, mx, NEG), jnp.where(y_b, my, NEG)))
        pa = jnp.exp2(sa - ma)
        pb = jnp.exp2(sb - mb)
        px = jnp.exp2(sx - jnp.where(x_b, mb, ma))
        py = jnp.exp2(sy - jnp.where(y_b, mb, ma))
        m_ref[g, 0] = ma
        m_ref[g, 1] = mb
        l_ref[g, 0] = fold(pa)
        l_ref[g, 1] = fold(pb)
        acc_ref[g, 0] = pv(pa, g, FIRST[0], 1)
        acc_ref[g, 1] = pv(pb, g, 0, 4)
        l_ref[g, sel_x] += fold(px)
        acc_ref[g, sel_x] += pv(px, g, tile_x, 1)
        l_ref[g, sel_y] += fold(py)
        acc_ref[g, sel_y] += pv(py, g, tile_y, 1)

    stores = [pltpu.make_async_copy(out_ref.at[rep * g:rep * (g + 1)], o_hbm.at[rep * g:rep * (g + 1)], out_sem.at[g])
              for g in range(ng)]

    def stage_b(g):
        sb = scores(queries(1, g), keys(g, 0, FIRST[3], 1))
        sd = scores(queries(sel_d, g), keys(g, 0, tile_d, 1))
        md = rowmax(sd)
        ma0, mb0 = m_ref[g, 0], m_ref[g, 1]
        ma = jnp.maximum(ma0, jnp.where(d_b, NEG, md))
        mb = jnp.maximum(jnp.maximum(mb0, rowmax(sb)), jnp.where(d_b, md, NEG))
        pb = jnp.exp2(sb - mb)
        pd = jnp.exp2(sd - jnp.where(d_b, mb, ma))
        al_a, al_b = jnp.exp2(ma0 - ma), jnp.exp2(mb0 - mb)
        l_ref[g, 0] = al_a * l_ref[g, 0]
        l_ref[g, 1] = al_b * l_ref[g, 1] + fold(pb)
        acc_ref[g, 0] = al_a * acc_ref[g, 0]
        acc_ref[g, 1] = al_b * acc_ref[g, 1] + pv(pb, g, FIRST[3], 1)
        l_ref[g, sel_d] += fold(pd)
        acc_ref[g, sel_d] += pv(pd, g, tile_d, 1)
        for s in range(2):
            l = jnp.sum(l_ref[g, s], axis=-1, keepdims=True)
            o = acc_ref[g, s] * (1.0 / l)
            out_ref[rep * g:rep * (g + 1), s * c:(s + 1) * c, :] = o.astype(jnp.bfloat16).reshape(rep, c, hd)
        stores[g].start()

    def direct(g):
        for h in range(2):
            for w in range(2):
                own[g][h][w].wait_recv()
                fwd[g][h][w].start()
            rel[g][h].start()

    def direct_done(g):
        for h in range(2):
            own[g][h][2].wait_recv()
            for w in range(2):
                fwd[g][h][w].wait_recv()

    def relayed(g):
        for h in range(2):
            rel[g][h].wait_recv()
            fwd[g][h][2].start()

    def relayed_done(g):
        for h in range(2):
            fwd[g][h][2].wait_recv()

    direct(0)
    for g in range(1, ng):
        direct(g)
        direct_done(g - 1)
        stage_a(g - 1)
    relayed(0)
    direct_done(ng - 1)
    stage_a(ng - 1)
    for g in range(1, ng):
        relayed(g)
        relayed_done(g - 1)
        stage_b(g - 1)
    relayed_done(ng - 1)
    stage_b(ng - 1)

    for g in range(ng):
        for h in range(2):
            for w in range(3):
                own[g][h][w].wait_send()
                fwd[g][h][w].wait_send()
            rel[g][h].wait_send()
        stores[g].wait()


def solution(mesh):
    spec = P(('dp', 'cy', 'cx'))

    def local(q, k, v):
        t, nh, hd = q.shape
        ng = k.shape[1]
        rep = nh // ng
        c = t // 2
        qt = q.transpose(1, 0, 2)
        any_spec = pl.BlockSpec(memory_space=pl.ANY)
        dma = pltpu.SemaphoreType.DMA
        o = pl.pallas_call(
            functools.partial(kernel, ng=ng, rep=rep, c=c, hd=hd),
            out_shape=jax.ShapeDtypeStruct((nh, t, hd), jnp.bfloat16),
            in_specs=[any_spec] * 3,
            out_specs=any_spec,
            scratch_shapes=[
                pltpu.VMEM((2, nh, c, hd), jnp.bfloat16),
                pltpu.VMEM((t * ng, hd), jnp.bfloat16),
                pltpu.VMEM((t * ng, hd), jnp.bfloat16),
                pltpu.VMEM((2, t * ng, hd), jnp.float32),
                pltpu.VMEM((ng, 8, 2, 2, c, hd), jnp.bfloat16),
                pltpu.VMEM((ng, 2, rep * c, 1), jnp.float32),
                pltpu.VMEM((ng, 2, rep * c, 128), jnp.float32),
                pltpu.VMEM((ng, 2, rep * c, hd), jnp.float32),
                pltpu.VMEM((nh, t, hd), jnp.bfloat16),
                dma((4,)), dma((ng,)),
                dma((ng, 2, 3)), dma((ng, 2, 3)),
                dma((ng, 2)), dma((ng, 2)),
                dma((ng, 2, 3)), dma((ng, 2, 3)),
            ],
            compiler_params=pltpu.CompilerParams(collective_id=0, has_side_effects=True),
        )(qt, k.reshape(t * ng, hd), v.reshape(t * ng, hd))
        return o.transpose(1, 0, 2)

    return jax.shard_map(local, mesh=mesh, in_specs=(spec, spec, spec), out_specs=spec, check_vma=False)
```

time: 58.5 us -> 21.8 us (0.37)
  matrix products: 22.7 us -> 0 us
  waiting for transfers between devices: 20.4 us -> 0 us
  Pallas kernels: 0 us -> 19.5 us
  starting transfers between devices: 5.99 us -> 0 us
  other arithmetic: 5.61 us -> 0 us
  local copies, waits for them, and re-layouts: 3.07 us -> 2.2 us
  between operations: 0.6 us -> 0.01 us
    dot_general x34 -> x0, matrix products: 22.7 us -> none  [the longest x17 13.9 us: update(): jnp.einsum('grqk,kgd->grqd', p.astype(jnp.bfloat16), vc, preferred_elemen...]
    ppermute x14 -> x0, waiting for transfers between devices: 20.4 us -> none  [the longest x7 11.7 us: local(): kb = lax.ppermute(kb, axes, perm)]
    pallas_call x0 -> x1, Pallas kernels: none -> 19.5 us  [local(): pl.pallas_call(functools.partial(kernel, ng=ng, rep=rep, c=c, hd=hd), out...]
    ppermute x14 -> x0, starting transfers between devices: 5.99 us -> none  [the longest x7 4.99 us: local(): vb = lax.ppermute(vb, axes, perm)]
    reduce_sum x10 -> x0, other arithmetic: 3.76 us -> none  [update(): l = alpha * l + jnp.sum(p, axis=-1)]
    slice x1 -> x0, local copies, waits for them, and re-layouts: 1.23 us -> none  [local(): qa = q[:c].reshape(c, value_a3, rep, hd)]
    concatenate x1 -> x0, other arithmetic: 0.98 us -> none  [local(): jnp.concatenate([finish(sa, c, nh, hd), finish(sb, c, nh, hd)], axis=0)]
    unnamed x2 -> x1, local copies, waits for them, and re-layouts: 1.85 us -> 2.2 us
  transfers between devices with their start and end apart: 14 -> 0, of which waited for: 9 -> 0; matrix products, arithmetic and copies ran while one was open for 45% -> 0% of each run, Pallas kernels for 0% -> 0%
where the time goes in v1:
time: 21.8 us; the launch traced here: 21.7 us
  Pallas kernels  19.5 us (89%)
  local copies, waits for them, and re-layouts  2.2 us (10%)
    pallas_call x1, Pallas kernels, local(): pl.pallas_call(functools.partial(kernel, ng=ng, rep=rep, c=c, hd=hd), out...  19.5 us
    unnamed x1, local copies, waits for them, and re-layouts  2.2 us

profile of v1, /device:TPU:0, one launch (start us, length us, event | category | flops | bytes accessed | tf_op | source)
XLA Modules:
  0.0 21.7 jit_solution(15754997276665508754)
XLA Ops:
  0.0 19.5 %shard_map.37 = bf16[28,128,128]{2,1,0:T(8,128)(2,1)} custom-call(bf16[28,128,128]{2,1,0:T(8,128)(2,1)} %bitcast.5, bf16[512,128]{1,0:T(8,128)(2,1)} %bitcast.6, bf16[512,128]{1,0:T(8,128)(2,1)} %bitcast.7), custom_call_target="tpu_custom_call" | custom-call | tf_op jit(solution)/shard_map/pallas_call | solution.py:221
  19.5 2.2 %copy.5 = bf16[128,28,128]{2,0,1:T(8,128)(2,1)} copy(bf16[128,28,128]{2,0,1:T(8,128)(2,1)} %bitcast.4) | data formatting | bytes 1835008

commit v2 on v1

--- a/solution.py
+++ b/solution.py
@@ -15,8 +15,8 @@
 SECOND = (0, 6, 7, 5)
 
 
-def kernel(q_hbm, k_hbm, v_hbm, o_hbm, qs, kin, vin, kf, g_ref, m_ref, l_ref, acc_ref, out_ref,
-           in_sem, out_sem, own_send, own_recv, rel_send, rel_recv, fwd_send, fwd_recv, *, ng, rep, c, hd):
+def kernel(q_hbm, k_hbm, v_hbm, out_ref, qs, kin, vin, kf, g_ref, m_ref, l_ref, acc_ref,
+           in_sem, own_send, own_recv, rel_send, rel_recv, fwd_send, fwd_recv, *, ng, rep, c, hd):
     icy = lax.axis_index('cy')
     icx = lax.axis_index('cx')
     core = icx % 2
@@ -136,9 +136,6 @@
         l_ref[g, sel_y] += fold(py)
         acc_ref[g, sel_y] += pv(py, g, tile_y, 1)
 
-    stores = [pltpu.make_async_copy(out_ref.at[rep * g:rep * (g + 1)], o_hbm.at[rep * g:rep * (g + 1)], out_sem.at[g])
-              for g in range(ng)]
-
     def stage_b(g):
         sb = scores(queries(1, g), keys(g, 0, FIRST[3], 1))
         sd = scores(queries(sel_d, g), keys(g, 0, tile_d, 1))
@@ -159,7 +156,6 @@
             l = jnp.sum(l_ref[g, s], axis=-1, keepdims=True)
             o = acc_ref[g, s] * (1.0 / l)
             out_ref[rep * g:rep * (g + 1), s * c:(s + 1) * c, :] = o.astype(jnp.bfloat16).reshape(rep, c, hd)
-        stores[g].start()
 
     def direct(g):
         for h in range(2):
@@ -204,7 +200,6 @@
                 own[g][h][w].wait_send()
                 fwd[g][h][w].wait_send()
             rel[g][h].wait_send()
-        stores[g].wait()
 
 
 def solution(mesh):
@@ -220,9 +215,9 @@
         dma = pltpu.SemaphoreType.DMA
         o = pl.pallas_call(
             functools.partial(kernel, ng=ng, rep=rep, c=c, hd=hd),
-            out_shape=jax.ShapeDtypeStruct((nh, t, hd), jnp.bfloat16),
+            out_shape=pltpu.VMEM((nh, t, hd), jnp.bfloat16),
             in_specs=[any_spec] * 3,
-            out_specs=any_spec,
+            out_specs=pl.BlockSpec(memory_space=pltpu.VMEM),
             scratch_shapes=[
                 pltpu.VMEM((2, nh, c, hd), jnp.bfloat16),
                 pltpu.VMEM((t * ng, hd), jnp.bfloat16),
@@ -232,8 +227,7 @@
                 pltpu.VMEM((ng, 2, rep * c, 1), jnp.float32),
                 pltpu.VMEM((ng, 2, rep * c, 128), jnp.float32),
                 pltpu.VMEM((ng, 2, rep * c, hd), jnp.float32),
-                pltpu.VMEM((nh, t, hd), jnp.bfloat16),
-                dma((4,)), dma((ng,)),
+                dma((4,)),
                 dma((ng, 2, 3)), dma((ng, 2, 3)),
                 dma((ng, 2)), dma((ng, 2)),
                 dma((ng, 2, 3)), dma((ng, 2, 3)),

time: 21.8 us -> 19.9 us (0.913)
  local copies, waits for them, and re-layouts: 2.2 us -> 0.93 us
  Pallas kernels: 19.5 us -> 18.9 us
    unnamed x1, local copies, waits for them, and re-layouts: 2.2 us -> 0.93 us
    pallas_call x1, Pallas kernels: 19.5 us -> 18.9 us  [local(): pl.pallas_call(functools.partial(kernel, ng=ng, rep=rep, c=c, hd=hd), out...]
where the time goes in v2:
time: 19.9 us; the launch traced here: 19.8 us
  Pallas kernels  18.9 us (95%)
  local copies, waits for them, and re-layouts  0.93 us (5%)
    pallas_call x1, Pallas kernels, local(): pl.pallas_call(functools.partial(kernel, ng=ng, rep=rep, c=c, hd=hd), out...  18.9 us
    unnamed x1, local copies, waits for them, and re-layouts  0.93 us

profile of v2, /device:TPU:0, one launch (start us, length us, event | category | flops | bytes accessed | tf_op | source)
XLA Modules:
  0.0 19.8 jit_solution(2263203080029078341)
XLA Ops:
  0.0 18.9 %shard_map.37 = bf16[28,128,128]{2,1,0:T(8,128)(2,1)S(1)} custom-call(bf16[28,128,128]{2,1,0:T(8,128)(2,1)} %bitcast.5, bf16[512,128]{1,0:T(8,128)(2,1)} %bitcast.6, bf16[512,128]{1,0:T(8,128)(2,1)} %bitcast.7), custom_call_target="tpu_custom_call" | custom-call | tf_op jit(solution)/shard_map/pallas_call | solution.py:216
  18.9 0.9 %copy.5 = bf16[128,28,128]{2,0,1:T(8,128)(2,1)} copy(bf16[128,28,128]{2,0,1:T(8,128)(2,1)S(1)} %bitcast.4) | data formatting | bytes 1835008

commit v3 on v0

v3 whole, which is shorter than its diff:
```python
import functools
import math

import jax
import jax.numpy as jnp
from jax import lax
from jax.experimental import pallas as pl
from jax.experimental.pallas import tpu as pltpu
from jax.sharding import PartitionSpec as P

NEG = -1.0e30
MESH = pl.DeviceIdType.MESH

S1, F1, F2, S2, S0, F0, S0B, F3, S3 = range(9)
TILES = 9
X, Y, SIB = 0, 1, 2
RX, RY = 2, 3

A_EARLY = (((F0, 1),), ((F1, 1), (F0, 1)), ((F2, 1), (F0, 1)), ((F1, 2), (F0, 1)))
B_EARLY = (((S1, 6),), ((F1, 5),), ((S1, 3), (S0, 2)), ((F1, 2), (S0, 2)))
A_LATE = ((), (), ((F3, 1),), ((F3, 1),))
B_LATE = (((F3, 2),), ((F3, 2),), ((F3, 1),), ((F3, 1),))


def kernel(q_hbm, k_hbm, v_hbm, out_ref, qs, kin, vin, kf, g_ref, m_ref, l_ref, acc_ref,
           in_sem, own_send, own_recv, rel_send, rel_recv, fwd_send, fwd_recv, here, *, ng, rep, c, hd):
    icy = lax.axis_index('cy')
    icx = lax.axis_index('cx')
    core = icx % 2
    chip_index = icy * 2 + icx // 2
    xdev = {'cx': (icx + 2) % 4}
    ydev = {'cy': (icy + 1) % 2}
    sdev = {'cx': icx + 1 - 2 * core}
    devs = (xdev, ydev, sdev)
    barrier = pltpu.get_barrier_semaphore()
    mul = math.log2(math.e) * hd ** -0.5

    def signal(sem, dev):
        pl.semaphore_signal(sem, inc=1, device_id=dev, device_id_type=MESH)

    def remote(src, dst, send, recv, dev):
        return pltpu.make_async_remote_copy(src_ref=src, dst_ref=dst, send_sem=send, recv_sem=recv,
                                            device_id=dev, device_id_type=MESH)

    def tiles(g, run, lane):
        return g_ref.at[g, :, pl.ds(run[0], run[1]), lane]

    class Copy:
        def __init__(self, g, src, dst, lane, send, recv, dev):
            self.cp = remote(tiles(g, src, 0), tiles(g, dst, lane), send, recv, dev)
            self.start = self.cp.start
            self.wait_send = self.cp.wait_send

    def arrival(g, run, lane, send, recv):
        remote(tiles(g, run, lane), tiles(g, run, lane), send, recv, sdev).wait_recv()

    loads = [
        pltpu.make_async_copy(k_hbm, kin, in_sem.at[0]),
        pltpu.make_async_copy(v_hbm, vin, in_sem.at[1]),
        pltpu.make_async_copy(q_hbm.at[:, 0:c, :], qs.at[0], in_sem.at[2]),
        pltpu.make_async_copy(q_hbm.at[:, c:2 * c, :], qs.at[1], in_sem.at[3]),
    ]
    for cp in loads:
        cp.start()

    @pl.when(chip_index == 0)
    def _():
        signal(barrier, xdev)
        signal(barrier, ydev)

    @pl.when(chip_index == 1)
    def _():
        signal(barrier, ydev)

    @pl.when(chip_index == 2)
    def _():
        signal(barrier, xdev)

    @pl.when(jnp.logical_or(core == 1, chip_index == 0))
    def _():
        signal(barrier, sdev)

    for t, src in enumerate((kin, vin)):
        loads[t].wait()
        kf[t] = src[...].astype(jnp.float32)
        for g in range(ng):
            x = kf[t, pl.ds(g, 2 * c, stride=ng), :].astype(jnp.bfloat16)
            g_ref[g, t, F0, 0] = x[:c]
            g_ref[g, t, S0, 0] = x[c:]
            g_ref[g, t, S0B, 0] = x[c:]

    known = jnp.where(chip_index == 0, 1, jnp.where(chip_index == 3, 3, 2) - core)
    pl.semaphore_wait(barrier, known)

    def run(chip):
        nx, ny, nd = chip ^ 1, chip ^ 2, chip ^ 3
        heads = range(ng)

        def own_runs(way):
            to = (nx, ny)[way]
            if to < chip:
                return ((S0, 2), (S1, 2)) if way == X else ((F0, 2), (F2, 2))
            return (F0, 1), ((F1, 1), (F2, 1))[way]

        def own_half(way, half):
            src = F0 if half == 0 else (S0 if way == X else S0B)
            dst = ((F1, S1), (F2, S2))[way][half]
            return (src, 1), (dst, 1)

        def own_list(way, frm, g):
            to = frm ^ (1, 2)[way]
            if to > frm:
                return [own_half(way, 0)]
            if frm == 3 and g >= 2:
                return [own_half(way, 0), own_half(way, 1)]
            return [((S0, 2), (S1, 2)) if way == X else ((F0, 2), (F2, 2))]

        def own_copies(way, g):
            return [Copy(g, s, d, 0, own_send.at[g, way, i], own_recv.at[g, way, i], devs[way])
                    for i, (s, d) in enumerate(own_list(way, chip, g))]

        own_x = [own_copies(X, g) for g in heads]
        own_y = [own_copies(Y, g) for g in heads]
        own_s = [[Copy(g, (S0, 2), (S0, 2), 1, own_send.at[g, SIB, 0], own_recv.at[g, SIB, 0], sdev)] for g in heads]

        def rel_run(way, frm, g):
            if way == Y:
                if frm == 2:
                    return (S1, 1), (S3, 1)
                if frm == 3 and g >= 2:
                    return None
                return (F1, 1), (F3, 1)
            if frm == 0:
                return ((S2, 1), (S3, 1)) if g < 2 else ((F2, 2), (F3, 2))
            if frm == 1:
                return (F2, 1), (F3, 1)
            return None

        def rel_copy(way, g):
            r = rel_run(way, chip, g)
            return None if r is None else Copy(g, r[0], r[1], 0, rel_send.at[g, way], rel_recv.at[g, way], devs[way])

        rels = [[rel_copy(w, g) for w in (X, Y)] for g in heads]

        def in_runs(way, g):
            return [d for _, d in own_list(way, (nx, ny)[way], g)]

        def rel_in(way, g):
            r = rel_run(way, (nx, ny)[way], g)
            return None if r is None else r[1]

        def fwd_copy(g, run_, way, i):
            return Copy(g, run_, run_, 1, fwd_send.at[g, way, i], fwd_recv.at[g, way, i], sdev)

        def start_all(copies):
            for cp in copies:
                cp.start()

        started = []

        def begin(cp):
            cp.start()
            started.append(cp)

        def wait_sends():
            for cp in started:
                cp.wait_send()
            started.clear()

        def send_own(way):
            lst = (own_x, own_y, own_s)[way]
            if chip == 3 and way < 2:
                first = way
                order = [(g, 0) for g in (0, 1)] + [(g, h if way == Y else 1 - h) for h in (0, 1) for g in (2, 3)]
                for g, i in order:
                    begin(lst[g][i])
            else:
                for g in heads:
                    for cp in lst[g]:
                        begin(cp)

        def sib_in():
            if chip:
                @pl.when(core == 1)
                def _():
                    pl.semaphore_wait(here.at[SIB], 1)

                @pl.when(core == 0)
                def _():
                    signal(here.at[SIB], sdev)

        if chip == 0:
            send_own(SIB)
            pl.semaphore_wait(here.at[X], 1)
            send_own(X)
            pl.semaphore_wait(here.at[Y], 1)
            send_own(Y)
        elif chip in (1, 2):
            back, on = (X, Y) if chip == 1 else (Y, X)
            send_own(back)
            signal(here.at[back], devs[back])
            sib_in()
            send_own(SIB)
            pl.semaphore_wait(here.at[on], 1)
            send_own(on)
        else:
            send_own(X)
            send_own(Y)
            signal(here.at[X], xdev)
            signal(here.at[Y], ydev)
            sib_in()
            send_own(SIB)
        for cp in loads[2:]:
            cp.wait()

        def direct(g):
            for way in (X, Y):
                for i, r in enumerate(in_runs(way, g)):
                    arrival(g, r, 0, own_send.at[g, way, i], own_recv.at[g, way, i])
                    begin(fwd_copy(g, r, way, i))
                other = Y if way == X else X
                if rels[g][other] is not None:
                    begin(rels[g][other])

        def direct_done(g):
            arrival(g, (S0, 2), 1, own_send.at[g, SIB, 0], own_recv.at[g, SIB, 0])
            for way in (X, Y):
                for i, r in enumerate(in_runs(way, g)):
                    arrival(g, r, 1, fwd_send.at[g, way, i], fwd_recv.at[g, way, i])

        def relayed(g):
            for way in (X, Y):
                r = rel_in(way, g)
                if r is not None:
                    arrival(g, r, 0, rel_send.at[g, way], rel_recv.at[g, way])
                    begin(fwd_copy(g, r, RX + way, 0))

        def relayed_done(g):
            for way in (X, Y):
                r = rel_in(way, g)
                if r is not None:
                    arrival(g, r, 1, fwd_send.at[g, RX + way, 0], fwd_recv.at[g, RX + way, 0])

        row = lax.broadcasted_iota(jnp.int32, (c, 2 * c), 0)
        col = lax.broadcasted_iota(jnp.int32, (c, 2 * c), 1)
        tri = col <= row
        masks = {F0: jnp.logical_or(tri, jnp.logical_and(col >= c, core == 1)),
                 S0: jnp.logical_or(tri, jnp.logical_and(col >= c, core == 0))}

        def queries(s, g):
            return qs[s, rep * g:rep * (g + 1)].reshape(rep * c, hd)

        def scores(s, g, runs, masked):
            out = []
            for first, count in runs:
                kk = g_ref[g, 0, first:first + count].reshape(count * 2 * c, hd)
                x = lax.dot_general(queries(s, g), kk, (((1,), (1,)), ((), ())), preferred_element_type=jnp.float32)
                for i in range(count):
                    y = x[:, i * 2 * c:(i + 1) * 2 * c] * mul
                    if first + i == masked:
                        y = jnp.where(masks[masked][None], y.reshape(rep, c, 2 * c), NEG).reshape(rep * c, 2 * c)
                    out.append(y)
            return out

        def rowmax(blocks):
            return jnp.max(functools.reduce(jnp.maximum, blocks), axis=-1, keepdims=True)

        def pv(p, g, runs):
            total, at = None, 0
            for first, count in runs:
                x = jnp.concatenate(p[at:at + count], axis=1).astype(jnp.bfloat16)
                y = jnp.dot(x, g_ref[g, 1, first:first + count].reshape(count * 2 * c, hd),
                            preferred_element_type=jnp.float32)
                total = y if total is None else total + y
                at += count
            return total

        def store(s, g, l, acc):
            o = acc * (1.0 / jnp.sum(l, axis=-1, keepdims=True))
            out_ref[rep * g:rep * (g + 1), s * c:(s + 1) * c, :] = o.astype(jnp.bfloat16).reshape(rep, c, hd)

        def early(s, g):
            runs = (A_EARLY, B_EARLY)[s][chip]
            sc = scores(s, g, runs, (F0, S0)[s])
            m = rowmax(sc)
            p = [jnp.exp2(x - m) for x in sc]
            l = functools.reduce(jnp.add, p)
            acc = pv(p, g, runs)
            if (A_LATE, B_LATE)[s][chip]:
                m_ref[g, s], l_ref[g, s], acc_ref[g, s] = m, l, acc
            else:
                store(s, g, l, acc)

        def late(s, g):
            runs = (A_LATE, B_LATE)[s][chip]
            if not runs:
                return
            sc = scores(s, g, runs, None)
            m0 = m_ref[g, s]
            m = jnp.maximum(m0, rowmax(sc))
            al = jnp.exp2(m0 - m)
            p = [jnp.exp2(x - m) for x in sc]
            l = functools.reduce(jnp.add, p) + al * l_ref[g, s]
            store(s, g, l, al * acc_ref[g, s] + pv(p, g, runs))

        def stage_a(g):
            early(0, g)
            early(1, g)

        def stage_b(g):
            late(0, g)
            late(1, g)

        direct(0)
        for g in range(1, ng):
            direct(g)
            direct_done(g - 1)
            stage_a(g - 1)
        relayed(0)
        direct_done(ng - 1)
        stage_a(ng - 1)
        for g in range(1, ng):
            relayed(g)
            relayed_done(g - 1)
            stage_b(g - 1)
        wait_sends()
        relayed_done(ng - 1)
        stage_b(ng - 1)

    for chip in range(4):
        pl.when(chip_index == chip)(functools.partial(run, chip))


def solution(mesh):
    spec = P(('dp', 'cy', 'cx'))

    def local(q, k, v):
        t, nh, hd = q.shape
        ng = k.shape[1]
        rep = nh // ng
        c = t // 2
        qt = q.transpose(1, 0, 2)
        any_spec = pl.BlockSpec(memory_space=pl.ANY)
        dma = pltpu.SemaphoreType.DMA
        o = pl.pallas_call(
            functools.partial(kernel, ng=ng, rep=rep, c=c, hd=hd),
            out_shape=pltpu.VMEM((nh, t, hd), jnp.bfloat16),
            in_specs=[any_spec] * 3,
            out_specs=pl.BlockSpec(memory_space=pltpu.VMEM),
            scratch_shapes=[
                pltpu.VMEM((2, nh, c, hd), jnp.bfloat16),
                pltpu.VMEM((t * ng, hd), jnp.bfloat16),
                pltpu.VMEM((t * ng, hd), jnp.bfloat16),
                pltpu.VMEM((2, t * ng, hd), jnp.float32),
                pltpu.VMEM((ng, 2, TILES, 2, c, hd), jnp.bfloat16),
                pltpu.VMEM((ng, 2, rep * c, 1), jnp.float32),
                pltpu.VMEM((ng, 2, rep * c, 128), jnp.float32),
                pltpu.VMEM((ng, 2, rep * c, hd), jnp.float32),
                dma((4,)),
                dma((ng, 3, 2)), dma((ng, 3, 2)),
                dma((ng, 2)), dma((ng, 2)),
                dma((ng, 4, 2)), dma((ng, 4, 2)),
                pltpu.SemaphoreType.REGULAR((3,)),
            ],
            compiler_params=pltpu.CompilerParams(collective_id=0, has_side_effects=True),
        )(qt, k.reshape(t * ng, hd), v.reshape(t * ng, hd))
        return o.transpose(1, 0, 2)

    return jax.shard_map(local, mesh=mesh, in_specs=(spec, spec, spec), out_specs=spec, check_vma=False)
```

time: 58.5 us -> 19.9 us (0.34)
  matrix products: 22.7 us -> 0 us
  waiting for transfers between devices: 20.4 us -> 0 us
  Pallas kernels: 0 us -> 18.8 us
  starting transfers between devices: 5.99 us -> 0 us
  other arithmetic: 5.61 us -> 0 us
  local copies, waits for them, and re-layouts: 3.07 us -> 0.93 us
  between operations: 0.6 us -> 0.01 us
    dot_general x34 -> x0, matrix products: 22.7 us -> none  [the longest x17 13.9 us: update(): jnp.einsum('grqk,kgd->grqd', p.astype(jnp.bfloat16), vc, preferred_elemen...]
    ppermute x14 -> x0, waiting for transfers between devices: 20.4 us -> none  [the longest x7 11.7 us: local(): kb = lax.ppermute(kb, axes, perm)]
    pallas_call x0 -> x1, Pallas kernels: none -> 18.8 us  [local(): pl.pallas_call(functools.partial(kernel, ng=ng, rep=rep, c=c, hd=hd), out...]
    ppermute x14 -> x0, starting transfers between devices: 5.99 us -> none  [the longest x7 4.99 us: local(): vb = lax.ppermute(vb, axes, perm)]
    reduce_sum x10 -> x0, other arithmetic: 3.76 us -> none  [update(): l = alpha * l + jnp.sum(p, axis=-1)]
    slice x1 -> x0, local copies, waits for them, and re-layouts: 1.23 us -> none  [local(): qa = q[:c].reshape(c, value_a3, rep, hd)]
    concatenate x1 -> x0, other arithmetic: 0.98 us -> none  [local(): jnp.concatenate([finish(sa, c, nh, hd), finish(sb, c, nh, hd)], axis=0)]
    unnamed x2 -> x1, local copies, waits for them, and re-layouts: 1.85 us -> 0.93 us
  transfers between devices with their start and end apart: 14 -> 0, of which waited for: 9 -> 0; matrix products, arithmetic and copies ran while one was open for 45% -> 0% of each run, Pallas kernels for 0% -> 0%
where the time goes in v3:
time: 19.9 us; the launch traced here: 19.8 us
  Pallas kernels  18.8 us (94%)
  local copies, waits for them, and re-layouts  0.93 us (5%)
    pallas_call x1, Pallas kernels, local(): pl.pallas_call(functools.partial(kernel, ng=ng, rep=rep, c=c, hd=hd), out...  18.8 us
    unnamed x1, local copies, waits for them, and re-layouts  0.93 us

profile of v3, /device:TPU:0, one launch (start us, length us, event | category | flops | bytes accessed | tf_op | source)
XLA Modules:
  0.0 19.8 jit_solution(10290473078287890296)
XLA Ops:
  0.0 18.8 %shard_map.37 = bf16[28,128,128]{2,1,0:T(8,128)(2,1)S(1)} custom-call(bf16[28,128,128]{2,1,0:T(8,128)(2,1)} %bitcast.5, bf16[512,128]{1,0:T(8,128)(2,1)} %bitcast.6, bf16[512,128]{1,0:T(8,128)(2,1)} %bitcast.7), custom_call_target="tpu_custom_call" | custom-call | tf_op jit(solution)/shard_map/pallas_call | solution.py:345
  18.9 0.9 %copy.5 = bf16[128,28,128]{2,0,1:T(8,128)(2,1)} copy(bf16[128,28,128]{2,0,1:T(8,128)(2,1)S(1)} %bitcast.4) | data formatting | bytes 1835008

commit v4 on v0

v4 whole, which is shorter than its diff:
```python
import functools
import math

import jax
import jax.numpy as jnp
from jax import lax
from jax.experimental import pallas as pl
from jax.experimental.pallas import tpu as pltpu
from jax.sharding import PartitionSpec as P

NEG = -1.0e30
MESH = pl.DeviceIdType.MESH

S1, F1, F2, S2, S0, F0, S0B, F3, S3 = range(9)
TILES = 9
X, Y, SIB = 0, 1, 2
RX, RY = 2, 3

NEAR = (((), ((F1, 1),), ((F2, 1),), ((F1, 2),)),
        (((S1, 4),), ((F1, 3),), ((S1, 3),), ((F1, 2),)))
FAR = (((), (), ((F3, 1),), ((F3, 1),)),
       (((F3, 2),), ((F3, 2),), ((F3, 1),), ((F3, 1),)))


def kernel(q_hbm, k_hbm, v_hbm, out_ref, qs, kin, vin, kf, g_ref, m_ref, l_ref, acc_ref,
           in_sem, own_send, own_recv, rel_send, rel_recv, fwd_send, fwd_recv, here, *, ng, rep, c, hd):
    icy = lax.axis_index('cy')
    icx = lax.axis_index('cx')
    core = icx % 2
    chip_index = icy * 2 + icx // 2
    xdev = {'cx': (icx + 2) % 4}
    ydev = {'cy': (icy + 1) % 2}
    sdev = {'cx': icx + 1 - 2 * core}
    devs = (xdev, ydev, sdev)
    barrier = pltpu.get_barrier_semaphore()
    mul = math.log2(math.e) * hd ** -0.5

    def signal(sem, dev):
        pl.semaphore_signal(sem, inc=1, device_id=dev, device_id_type=MESH)

    def remote(src, dst, send, recv, dev):
        return pltpu.make_async_remote_copy(src_ref=src, dst_ref=dst, send_sem=send, recv_sem=recv,
                                            device_id=dev, device_id_type=MESH)

    def tiles(g, run, lane):
        return g_ref.at[g, :, pl.ds(run[0], run[1]), lane]

    class Copy:
        def __init__(self, g, src, dst, lane, send, recv, dev):
            self.cp = remote(tiles(g, src, 0), tiles(g, dst, lane), send, recv, dev)
            self.start = self.cp.start
            self.wait_send = self.cp.wait_send

    def arrival(g, run, lane, send, recv):
        remote(tiles(g, run, lane), tiles(g, run, lane), send, recv, sdev).wait_recv()

    loads = [
        pltpu.make_async_copy(k_hbm, kin, in_sem.at[0]),
        pltpu.make_async_copy(v_hbm, vin, in_sem.at[1]),
        pltpu.make_async_copy(q_hbm.at[:, 0:c, :], qs.at[0], in_sem.at[2]),
        pltpu.make_async_copy(q_hbm.at[:, c:2 * c, :], qs.at[1], in_sem.at[3]),
    ]
    for cp in loads:
        cp.start()

    @pl.when(chip_index == 0)
    def _():
        signal(barrier, xdev)
        signal(barrier, ydev)

    @pl.when(chip_index == 1)
    def _():
        signal(barrier, ydev)

    @pl.when(chip_index == 2)
    def _():
        signal(barrier, xdev)

    @pl.when(jnp.logical_or(core == 1, chip_index == 0))
    def _():
        signal(barrier, sdev)

    for t, src in enumerate((kin, vin)):
        loads[t].wait()
        kf[t] = src[...].astype(jnp.float32)
        for g in range(ng):
            x = kf[t, pl.ds(g, 2 * c, stride=ng), :].astype(jnp.bfloat16)
            g_ref[g, t, F0, 0] = x[:c]
            g_ref[g, t, S0, 0] = x[c:]
            g_ref[g, t, S0B, 0] = x[c:]

    known = jnp.where(chip_index == 0, 1, jnp.where(chip_index == 3, 3, 2) - core)
    pl.semaphore_wait(barrier, known)

    row = lax.broadcasted_iota(jnp.int32, (c, 2 * c), 0)
    col = lax.broadcasted_iota(jnp.int32, (c, 2 * c), 1)
    tri = col <= row
    masks = {F0: jnp.logical_or(tri, jnp.logical_and(col >= c, core == 1)),
             S0: jnp.logical_or(tri, jnp.logical_and(col >= c, core == 0))}

    def scores(s, g, runs, masked):
        q = qs[s, pl.ds(rep * g, rep)].reshape(rep * c, hd)
        out = []
        for first, count in runs:
            kk = g_ref[g, 0, first:first + count].reshape(count * 2 * c, hd)
            x = lax.dot_general(q, kk, (((1,), (1,)), ((), ())), preferred_element_type=jnp.float32)
            for i in range(count):
                y = x[:, i * 2 * c:(i + 1) * 2 * c] * mul
                if first + i == masked:
                    y = jnp.where(masks[masked][None], y.reshape(rep, c, 2 * c), NEG).reshape(rep * c, 2 * c)
                out.append(y)
        return out

    def rowmax(blocks):
        m = jnp.max(functools.reduce(jnp.maximum, blocks), axis=-1, keepdims=True)
        return jnp.broadcast_to(m, (rep * c, 2 * c))

    def pv(p, g, runs):
        total, at = None, 0
        for first, count in runs:
            x = jnp.concatenate(p[at:at + count], axis=1).astype(jnp.bfloat16)
            y = jnp.dot(x, g_ref[g, 1, first:first + count].reshape(count * 2 * c, hd),
                        preferred_element_type=jnp.float32)
            total = y if total is None else total + y
            at += count
        return total

    def attend(s, g, runs, first, last, masked=None):
        if not runs:
            return
        sc = scores(s, g, runs, masked)
        m = rowmax(sc)
        if not first:
            m0 = m_ref[g, s]
            m = jnp.maximum(m0, m)
            al = jnp.exp2(m0 - m)
        p = [jnp.exp2(x - m) for x in sc]
        l = functools.reduce(jnp.add, p)
        acc = pv(p, g, runs)
        if not first:
            l += al * l_ref[g, s]
            acc += al * acc_ref[g, s]
        if last:
            o = acc * (1.0 / jnp.sum(l, axis=-1, keepdims=True))
            out_ref[pl.ds(rep * g, rep), s * c:(s + 1) * c, :] = o.astype(jnp.bfloat16).reshape(rep, c, hd)
        else:
            m_ref[g, s], l_ref[g, s], acc_ref[g, s] = m, l, acc

    def local(lo, hi):
        def body(g, carry):
            attend(0, g, ((F0, 1),), True, False, F0)
            attend(1, g, ((S0, 2),), True, False, S0)
            return carry

        lax.fori_loop(lo, hi, body, 0)

    heads = range(ng)

    def own_list(way, frm):
        f = (F0, 1), ((F1, 1), (F2, 1))[way]
        if frm ^ (1, 2)[way] > frm:
            return [f]
        if frm == 3:
            return [f, ((S0, 1), ((S1, 1), (S2, 1))[way])]
        return [((S0, 2), (S1, 2)) if way == X else ((F0, 2), (F2, 2))]

    def own_copy(way, frm, g, i):
        s, d = own_list(way, frm)[i]
        return Copy(g, s, d, 0, own_send.at[g, way, i], own_recv.at[g, way, i], devs[way])

    def own_sib(g):
        return Copy(g, (S0, 2), (S0, 2), 1, own_send.at[g, SIB, 0], own_recv.at[g, SIB, 0], sdev)

    def rel_run(way, frm, g):
        if way == Y:
            if frm == 2:
                return (S1, 1), (S3, 1)
            if frm == 3 and g >= 2:
                return None
            return (F1, 1), (F3, 1)
        if frm == 0:
            return ((S2, 1), (S3, 1)) if g < 2 else ((F2, 2), (F3, 2))
        if frm == 1:
            return (F2, 1), (F3, 1)
        return None

    def fwd_copy(g, run_, way, i):
        return Copy(g, run_, run_, 1, fwd_send.at[g, way, i], fwd_recv.at[g, way, i], sdev)

    def begin_all(copies):
        for cp in copies:
            cp.start()

    def own_order(way, frm):
        if frm == 3:
            return [(g, i) for i in ((1, 0) if way == X else (0, 1)) for g in heads]
        return [(g, 0) for g in heads]

    def send_own(way, chip):
        for g, i in own_order(way, chip):
            own_copy(way, chip, g, i).start()

    def send_sib():
        for g in heads:
            own_sib(g).start()

    def sib_in():
        @pl.when(core == 1)
        def _():
            pl.semaphore_wait(here.at[SIB], 1)

        @pl.when(core == 0)
        def _():
            signal(here.at[SIB], sdev)

    BACK = (None, X, Y, None)
    ON = (None, Y, X, None)

    def start_sends(chip):
        if chip in (1, 2):
            send_own(BACK[chip], chip)
            signal(here.at[BACK[chip]], devs[BACK[chip]])
        elif chip == 3:
            for a, b in zip(own_order(X, 3), own_order(Y, 3)):
                own_copy(X, 3, *a).start()
                own_copy(Y, 3, *b).start()
            signal(here.at[X], xdev)
            signal(here.at[Y], ydev)
        if chip:
            sib_in()
        send_sib()

    def later_sends(chip):
        for way in ((X, Y) if chip == 0 else (ON[chip],) if chip < 3 else ()):
            pl.semaphore_wait(here.at[way], 1)
            send_own(way, chip)

    def run(chip):
        nx, ny = chip ^ 1, chip ^ 2

        def take(way, g, i=0):
            r = own_list(way, (nx, ny)[way])[i][1]
            arrival(g, r, 0, own_send.at[g, way, i], own_recv.at[g, way, i])
            other = 1 - way
            rel = rel_run(other, chip, g)
            if rel is not None and r[0] <= rel[0][0] and rel[0][0] + rel[0][1] <= r[0] + r[1]:
                Copy(g, rel[0], rel[1], 0, rel_send.at[g, other], rel_recv.at[g, other], devs[other]).start()
            fwd_copy(g, r, way, i).start()

        def near_done(g):
            for way in (X, Y):
                for i, (_, r) in enumerate(own_list(way, (nx, ny)[way])):
                    arrival(g, r, 1, fwd_send.at[g, way, i], fwd_recv.at[g, way, i])

        def rel_in(way, g):
            r = rel_run(way, (nx, ny)[way], g)
            return None if r is None else r[1]

        def relayed(g):
            for way in (X, Y):
                r = rel_in(way, g)
                if r is not None:
                    arrival(g, r, 0, rel_send.at[g, way], rel_recv.at[g, way])
                    fwd_copy(g, r, RX + way, 0).start()

        def far_done(g):
            for way in (X, Y):
                r = rel_in(way, g)
                if r is not None:
                    arrival(g, r, 1, fwd_send.at[g, RX + way, 0], fwd_recv.at[g, RX + way, 0])

        def wait_sends():
            for g in heads:
                own_sib(g).wait_send()
                for way in (X, Y):
                    for i in range(len(own_list(way, chip))):
                        own_copy(way, chip, g, i).wait_send()
                    for i, (_, r) in enumerate(own_list(way, (nx, ny)[way])):
                        fwd_copy(g, r, way, i).wait_send()
                    rel = rel_run(way, chip, g)
                    if rel is not None:
                        Copy(g, rel[0], rel[1], 0, rel_send.at[g, way], rel_recv.at[g, way], devs[way]).wait_send()
                    r = rel_in(way, g)
                    if r is not None:
                        fwd_copy(g, r, RX + way, 0).wait_send()

        def near(g):
            near_done(g)
            attend(0, g, NEAR[0][chip], False, not FAR[0][chip])
            attend(1, g, NEAR[1][chip], False, False)

        def far(g):
            far_done(g)
            attend(0, g, FAR[0][chip], False, True)
            attend(1, g, FAR[1][chip], False, True)

        def finish_own(g):
            if not NEAR[0][chip] and not FAR[0][chip]:
                o = acc_ref[g, 0] * (1.0 / jnp.sum(l_ref[g, 0], axis=-1, keepdims=True))
                out_ref[rep * g:rep * (g + 1), :c, :] = o.astype(jnp.bfloat16).reshape(rep, c, hd)

        def both(way, g):
            for i in range(len(own_list(way, (nx, ny)[way]))):
                take(way, g, i)

        def on_core(k, *fns):
            @pl.when(core == k)
            def _():
                for f in fns:
                    f()

        part = functools.partial
        if chip == 0:
            for g in heads:
                finish_own(g)
            both(X, 0), both(Y, 0)
            for g in range(1, ng):
                both(X, g), both(Y, g)
                near(g - 1)
            on_core(0, part(relayed, 0))
            on_core(1, part(relayed, 0), part(relayed, 1))
            near(3)
            on_core(0, part(relayed, 1))
            on_core(1, part(relayed, 2))
            far(0)
            on_core(1, part(relayed, 3))
            far(1)
            on_core(0, part(relayed, 2))
            far(2)
            on_core(0, part(relayed, 3))
            wait_sends()
            far(3)
            return
        if chip == 1:
            for w, g in ((Y, 0), (Y, 1), (X, 0), (Y, 2), (X, 1), (Y, 3), (X, 2), (X, 3)):
                take(w, g)
            rest = [part(take, Y, g, 1) for g in heads]
        elif chip == 2:
            for w, g in ((X, 0), (X, 1), (Y, 0), (X, 2), (Y, 1), (X, 3), (Y, 2), (Y, 3)):
                take(w, g, 1 if w == X else 0)
            rest = [part(take, X, g, 0) for g in heads]
        else:
            rest = [lambda g=g: (take(X, g), take(Y, g)) for g in heads]
        rest[0]()
        for g in range(1, ng):
            rest[g]()
            near(g - 1)
        relayed(0)
        near(3)
        for g in range(1, ng):
            relayed(g)
            far(g - 1)
        wait_sends()
        far(3)

    def each_chip(f):
        for chip in range(4):
            pl.when(chip_index == chip)(functools.partial(f, chip))

    each_chip(start_sends)
    for cp in loads[2:]:
        cp.wait()
    for g in heads:
        arrival(g, (S0, 2), 1, own_send.at[g, SIB, 0], own_recv.at[g, SIB, 0])
    local(0, ng // 2)
    each_chip(later_sends)
    local(ng // 2, ng)
    each_chip(run)


def solution(mesh):
    spec = P(('dp', 'cy', 'cx'))

    def local(q, k, v):
        t, nh, hd = q.shape
        ng = k.shape[1]
        rep = nh // ng
        c = t // 2
        qt = q.transpose(1, 0, 2)
        any_spec = pl.BlockSpec(memory_space=pl.ANY)
        dma = pltpu.SemaphoreType.DMA
        o = pl.pallas_call(
            functools.partial(kernel, ng=ng, rep=rep, c=c, hd=hd),
            out_shape=pltpu.VMEM((nh, t, hd), jnp.bfloat16),
            in_specs=[any_spec] * 3,
            out_specs=pl.BlockSpec(memory_space=pltpu.VMEM),
            scratch_shapes=[
                pltpu.VMEM((2, nh, c, hd), jnp.bfloat16),
                pltpu.VMEM((t * ng, hd), jnp.bfloat16),
                pltpu.VMEM((t * ng, hd), jnp.bfloat16),
                pltpu.VMEM((2, t * ng, hd), jnp.float32),
                pltpu.VMEM((ng, 2, TILES, 2, c, hd), jnp.bfloat16),
                pltpu.VMEM((ng, 2, rep * c, 2 * c), jnp.float32),
                pltpu.VMEM((ng, 2, rep * c, 2 * c), jnp.float32),
                pltpu.VMEM((ng, 2, rep * c, hd), jnp.float32),
                dma((4,)),
                dma((ng, 3, 2)), dma((ng, 3, 2)),
                dma((ng, 2)), dma((ng, 2)),
                dma((ng, 4, 2)), dma((ng, 4, 2)),
                pltpu.SemaphoreType.REGULAR((3,)),
            ],
            compiler_params=pltpu.CompilerParams(collective_id=0, has_side_effects=True),
        )(qt, k.reshape(t * ng, hd), v.reshape(t * ng, hd))
        return o.transpose(1, 0, 2)

    return jax.shard_map(local, mesh=mesh, in_specs=(spec, spec, spec), out_specs=spec, check_vma=False)
```

time: 58.5 us -> 18.7 us (0.32)
  matrix products: 22.7 us -> 0 us
  waiting for transfers between devices: 20.4 us -> 0 us
  Pallas kernels: 0 us -> 17.6 us
  starting transfers between devices: 5.99 us -> 0 us
  other arithmetic: 5.61 us -> 0 us
  local copies, waits for them, and re-layouts: 3.07 us -> 0.93 us
  between operations: 0.6 us -> 0.01 us
    dot_general x34 -> x0, matrix products: 22.7 us -> none  [the longest x17 13.9 us: update(): jnp.einsum('grqk,kgd->grqd', p.astype(jnp.bfloat16), vc, preferred_elemen...]
    ppermute x14 -> x0, waiting for transfers between devices: 20.4 us -> none  [the longest x7 11.7 us: local(): kb = lax.ppermute(kb, axes, perm)]
    pallas_call x0 -> x1, Pallas kernels: none -> 17.6 us  [local(): pl.pallas_call(functools.partial(kernel, ng=ng, rep=rep, c=c, hd=hd), out...]
    ppermute x14 -> x0, starting transfers between devices: 5.99 us -> none  [the longest x7 4.99 us: local(): vb = lax.ppermute(vb, axes, perm)]
    reduce_sum x10 -> x0, other arithmetic: 3.76 us -> none  [update(): l = alpha * l + jnp.sum(p, axis=-1)]
    slice x1 -> x0, local copies, waits for them, and re-layouts: 1.23 us -> none  [local(): qa = q[:c].reshape(c, value_a3, rep, hd)]
    concatenate x1 -> x0, other arithmetic: 0.98 us -> none  [local(): jnp.concatenate([finish(sa, c, nh, hd), finish(sb, c, nh, hd)], axis=0)]
    unnamed x2 -> x1, local copies, waits for them, and re-layouts: 1.85 us -> 0.93 us
  transfers between devices with their start and end apart: 14 -> 0, of which waited for: 9 -> 0; matrix products, arithmetic and copies ran while one was open for 45% -> 0% of each run, Pallas kernels for 0% -> 0%
where the time goes in v4:
time: 18.7 us; the launch traced here: 18.6 us
  Pallas kernels  17.6 us (94%)
  local copies, waits for them, and re-layouts  0.93 us (5%)
    pallas_call x1, Pallas kernels, local(): pl.pallas_call(functools.partial(kernel, ng=ng, rep=rep, c=c, hd=hd), out...  17.6 us
    unnamed x1, local copies, waits for them, and re-layouts  0.93 us

profile of v4, /device:TPU:0, one launch (start us, length us, event | category | flops | bytes accessed | tf_op | source)
XLA Modules:
  0.0 18.6 jit_solution(7141355510928423346)
XLA Ops:
  0.0 17.6 %shard_map.37 = bf16[28,128,128]{2,1,0:T(8,128)(2,1)S(1)} custom-call(bf16[28,128,128]{2,1,0:T(8,128)(2,1)} %bitcast.5, bf16[512,128]{1,0:T(8,128)(2,1)} %bitcast.6, bf16[512,128]{1,0:T(8,128)(2,1)} %bitcast.7), custom_call_target="tpu_custom_call" | custom-call | tf_op jit(solution)/shard_map/pallas_call | solution.py:382
  17.6 0.9 %copy.5 = bf16[128,28,128]{2,0,1:T(8,128)(2,1)} copy(bf16[128,28,128]{2,0,1:T(8,128)(2,1)S(1)} %bitcast.4) | data formatting | bytes 1835008

commit v5 on v4

v5 whole, which is shorter than its diff:
```python
import functools
import math

import jax
import jax.numpy as jnp
from jax import lax
from jax.experimental import pallas as pl
from jax.experimental.pallas import tpu as pltpu
from jax.sharding import PartitionSpec as P

NEG = -1.0e30
MESH = pl.DeviceIdType.MESH

S1, F1, F2, S2, S0, F0, S0B, F3, S3 = range(9)
TILES = 9
X, Y, SIB = 0, 1, 2

NEAR = (((), ((F1, 1),), ((F2, 1),), ((F1, 2),)),
        (((S1, 4),), ((F1, 2),), ((S1, 1), (F2, 1)), ((F1, 2),)))
FAR = (((), (), ((F3, 1),), ((F3, 1),)),
       (((F3, 2),), ((S2, 1), (F3, 2)), ((F1, 1), (F3, 1)), ((F3, 1),)))

GROUP = (((0,), (0,)), ((1,), (0, 2)), ((2, 0), (1,)), ((0,), (0,)))
GROUP_RUN = (((S1, 4),), ((F2, 1), (F1, 1), (S2, 1)), ((S1, 1), (F2, 1), (F1, 1)), ((F1, 2),))
LATE = 2
NEAR_UNITS = (4, 2, 2, 2)
FAR_UNITS = (2, 3, 2, 1)
RELAYED = ((F3, 2), (F3, 2), (F3, 1), (F3, 1))


def kernel(q_hbm, k_hbm, v_hbm, out_ref, qs, kin, vin, kf, g_ref, m_ref, l_ref, acc_ref,
           in_sem, own_send, rel_send, fwd_send, sib_recv, msg_recv, rel_recv, fwd_recv, here, *, ng, rep, c, hd):
    icy = lax.axis_index('cy')
    icx = lax.axis_index('cx')
    core = icx % 2
    chip_index = icy * 2 + icx // 2
    xdev = {'cx': (icx + 2) % 4}
    ydev = {'cy': (icy + 1) % 2}
    sdev = {'cx': icx + 1 - 2 * core}
    devs = (xdev, ydev, sdev)
    barrier = pltpu.get_barrier_semaphore()
    mul = math.log2(math.e) * hd ** -0.5

    def signal(sem, dev):
        pl.semaphore_signal(sem, inc=1, device_id=dev, device_id_type=MESH)

    def remote(src, dst, send, recv, dev):
        return pltpu.make_async_remote_copy(src_ref=src, dst_ref=dst, send_sem=send, recv_sem=recv,
                                            device_id=dev, device_id_type=MESH)

    def tiles(g, run, lane):
        return g_ref.at[g, :, pl.ds(run[0], run[1]), lane]

    def copy(g, src, dst, lane, send, recv, dev):
        return remote(tiles(g, src, 0), tiles(g, dst, lane), send, recv, dev)

    def arrival(g, run, lane, recv):
        remote(tiles(g, run, lane), tiles(g, run, lane), own_send.at[0], recv, sdev).wait_recv()

    def sent(count, units, send):
        ref = g_ref.at[pl.ds(0, count), :, pl.ds(0, units), 0]
        remote(ref, ref, send, sib_recv.at[0], sdev).wait_send()

    loads = [
        pltpu.make_async_copy(k_hbm, kin, in_sem.at[0]),
        pltpu.make_async_copy(v_hbm, vin, in_sem.at[1]),
        pltpu.make_async_copy(q_hbm, qs, in_sem.at[2]),
    ]
    for cp in loads:
        cp.start()

    @pl.when(chip_index == 0)
    def _():
        signal(barrier, xdev)
        signal(barrier, ydev)

    @pl.when(chip_index == 1)
    def _():
        signal(barrier, ydev)

    @pl.when(chip_index == 2)
    def _():
        signal(barrier, xdev)

    @pl.when(jnp.logical_or(core == 1, chip_index == 0))
    def _():
        signal(barrier, sdev)

    for t, src in enumerate((kin, vin)):
        loads[t].wait()
        kf[t] = src[...].astype(jnp.float32)
        for g in range(ng):
            x = kf[t, pl.ds(g, 2 * c, stride=ng), :].astype(jnp.bfloat16)
            g_ref[g, t, F0, 0] = x[:c]
            g_ref[g, t, S0, 0] = x[c:]
            g_ref[g, t, S0B, 0] = x[c:]

    known = jnp.where(chip_index == 0, 1, jnp.where(chip_index == 3, 3, 2) - core)
    pl.semaphore_wait(barrier, known)

    row = lax.broadcasted_iota(jnp.int32, (c, 2 * c), 0)
    col = lax.broadcasted_iota(jnp.int32, (c, 2 * c), 1)
    tri = col <= row
    masks = {F0: jnp.logical_or(tri, jnp.logical_and(col >= c, core == 1)),
             S0: jnp.logical_or(tri, jnp.logical_and(col >= c, core == 0))}

    def scores(s, g, runs, masked):
        q = qs[pl.ds(rep * g, rep), s * c:(s + 1) * c].reshape(rep * c, hd)
        out = []
        for first, count in runs:
            kk = g_ref[g, 0, first:first + count].reshape(count * 2 * c, hd)
            x = lax.dot_general(q, kk, (((1,), (1,)), ((), ())), preferred_element_type=jnp.float32)
            for i in range(count):
                y = x[:, i * 2 * c:(i + 1) * 2 * c] * mul
                if first + i == masked:
                    y = jnp.where(masks[masked][None], y.reshape(rep, c, 2 * c), NEG).reshape(rep * c, 2 * c)
                out.append(y)
        return out

    def rowmax(blocks):
        m = jnp.max(functools.reduce(jnp.maximum, blocks), axis=-1, keepdims=True)
        return jnp.broadcast_to(m, (rep * c, 2 * c))

    def pv(p, g, runs):
        total, at = None, 0
        for first, count in runs:
            x = jnp.concatenate(p[at:at + count], axis=1).astype(jnp.bfloat16)
            y = jnp.dot(x, g_ref[g, 1, first:first + count].reshape(count * 2 * c, hd),
                        preferred_element_type=jnp.float32)
            total = y if total is None else total + y
            at += count
        return total

    def attend(s, g, runs, first, last, masked=None):
        if not runs:
            return
        sc = scores(s, g, runs, masked)
        m = rowmax(sc)
        if not first:
            m0 = m_ref[g, s]
            m = jnp.maximum(m0, m)
            al = jnp.exp2(m0 - m)
        p = [jnp.exp2(x - m) for x in sc]
        l = functools.reduce(jnp.add, p)
        acc = pv(p, g, runs)
        if not first:
            l += al * l_ref[g, s]
            acc += al * acc_ref[g, s]
        if last:
            o = acc * (1.0 / jnp.sum(l, axis=-1, keepdims=True))
            out_ref[pl.ds(rep * g, rep), s * c:(s + 1) * c, :] = o.astype(jnp.bfloat16).reshape(rep, c, hd)
        else:
            m_ref[g, s], l_ref[g, s], acc_ref[g, s] = m, l, acc

    def local(lo, hi):
        def body(g, carry):
            attend(0, g, ((F0, 1),), True, False, F0)
            attend(1, g, ((S0, 2),), True, False, S0)
            return carry

        lax.fori_loop(lo, hi, body, 0)

    heads = range(ng)

    def own_list(way, frm):
        f = (F0, 1), ((F1, 1), (F2, 1))[way]
        if frm ^ (1, 2)[way] > frm:
            return [f]
        if frm == 3:
            return [f, ((S0, 1), ((S1, 1), (S2, 1))[way])]
        return [((S0, 2), (S1, 2)) if way == X else ((F0, 2), (F2, 2))]

    def own_copy(way, frm, g, i):
        to = frm ^ (1, 2)[way]
        src, dst = own_list(way, frm)[i]
        return copy(g, src, dst, 0, own_send.at[way], msg_recv.at[g, GROUP[to][way][i]], devs[way])

    def rel_run(way, frm, g):
        if way == Y:
            if frm == 2:
                return (S1, 1), (S3, 1)
            if frm == 3 and g >= 2:
                return None
            return (F1, 1), (F3, 1)
        if frm == 0:
            return ((S2, 1), (S3, 1)) if g < 2 else ((F2, 2), (F3, 2))
        if frm == 1:
            return (F2, 1), (F3, 1)
        return None

    def forward(g, run_, send, recv):
        copy(g, run_, run_, 1, send, recv, sdev).start()

    def send_own(way, chip):
        late_first = chip == 3 and way == X
        count = len(own_list(way, chip))
        for i in (reversed(range(count)) if late_first else range(count)):
            for g in heads:
                own_copy(way, chip, g, i).start()

    def start_sends(chip):
        back, on = (None, X, Y, None)[chip], (None, Y, X, None)[chip]
        if back is not None:
            signal(here.at[back], devs[back])
            send_own(back, chip)
        elif chip == 3:
            signal(here.at[X], xdev)
            signal(here.at[Y], ydev)
            send_own(Y, chip)
            send_own(X, chip)
        if chip:
            @pl.when(core == 0)
            def _():
                signal(here.at[SIB], sdev)

            @pl.when(core == 1)
            def _():
                pl.semaphore_wait(here.at[SIB], 1)
        for g in heads:
            copy(g, (S0, 2), (S0, 2), 1, own_send.at[SIB], sib_recv.at[0], sdev).start()
        if on is not None:
            pl.semaphore_wait(here.at[on], 1)
            send_own(on, chip)

    def run(chip):
        def take(g, group):
            r = GROUP_RUN[chip][group]
            arrival(g, r, 0, msg_recv.at[g, group])
            for way in (X, Y):
                rel = rel_run(way, chip, g)
                if rel is not None and r[0] <= rel[0][0] and rel[0][0] + rel[0][1] <= r[0] + r[1]:
                    copy(g, rel[0], rel[1], 0, rel_send.at[way], rel_recv.at[g], devs[way]).start()
            stage = 1 if group == LATE else 0
            forward(g, r, fwd_send.at[stage], fwd_recv.at[g, stage])

        def relayed(g):
            arrival(g, RELAYED[chip], 0, rel_recv.at[g])
            forward(g, RELAYED[chip], fwd_send.at[1], fwd_recv.at[g, 1])

        def near(g):
            arrival(g, (0, NEAR_UNITS[chip]), 1, fwd_recv.at[g, 0])
            attend(0, g, NEAR[0][chip], False, not FAR[0][chip])
            attend(1, g, NEAR[1][chip], False, False)

        def far(g):
            arrival(g, (0, FAR_UNITS[chip]), 1, fwd_recv.at[g, 1])
            attend(0, g, FAR[0][chip], False, True)
            attend(1, g, FAR[1][chip], False, True)

        def finish_own(g):
            o = acc_ref[g, 0] * (1.0 / jnp.sum(l_ref[g, 0], axis=-1, keepdims=True))
            out_ref[rep * g:rep * (g + 1), :c, :] = o.astype(jnp.bfloat16).reshape(rep, c, hd)

        def wait_sends():
            sent(ng, 2, own_send.at[SIB])
            for way in (X, Y):
                sent(ng, sum(d[1] for _, d in own_list(way, chip)), own_send.at[way])
                rel = [rel_run(way, chip, g) for g in heads]
                units = sum(r[0][1] for r in rel if r is not None)
                if units:
                    count = 2 if units % ng else ng
                    sent(count, units // count, rel_send.at[way])
            sent(ng, NEAR_UNITS[chip], fwd_send.at[0])

        def on_core(k, *fns):
            @pl.when(core == k)
            def _():
                for f in fns:
                    f()

        part = functools.partial
        if chip == 0:
            for g in heads:
                finish_own(g)
            take(0, 0)
            for g in range(1, ng):
                take(g, 0)
                near(g - 1)
            on_core(0, part(relayed, 0))
            on_core(1, part(relayed, 0), part(relayed, 1))
            near(3)
            on_core(0, part(relayed, 1))
            on_core(1, part(relayed, 2))
            far(0)
            on_core(1, part(relayed, 3))
            far(1)
            wait_sends()
            on_core(0, part(relayed, 2))
            far(2)
            on_core(0, part(relayed, 3))
            far(3)
        elif chip == 3:
            take(0, 0)
            for g in range(1, ng):
                take(g, 0)
                near(g - 1)
            relayed(0)
            near(3)
            for g in range(1, ng):
                relayed(g)
                far(g - 1)
            wait_sends()
            far(3)
        else:
            for g, group in ((0, 0), (1, 0), (0, 1), (2, 0), (1, 1), (3, 0)):
                take(g, group)
            near(0)
            take(2, 1), take(3, 1)
            near(1)
            take(0, LATE), take(1, LATE)
            near(2)
            take(2, LATE), relayed(0)
            near(3)
            take(3, LATE), relayed(1)
            far(0)
            relayed(2)
            far(1)
            wait_sends()
            relayed(3)
            far(2)
            far(3)
        sent(ng, FAR_UNITS[chip], fwd_send.at[1])

    def each_chip(f):
        for chip in range(4):
            pl.when(chip_index == chip)(functools.partial(f, chip))

    each_chip(start_sends)
    loads[2].wait()
    own = g_ref.at[:, :, pl.ds(S0, 2), 1]
    remote(own, own, own_send.at[SIB], sib_recv.at[0], sdev).wait_recv()
    local(0, ng // 2)

    @pl.when(chip_index == 0)
    def _():
        for way in (X, Y):
            pl.semaphore_wait(here.at[way], 1)
            send_own(way, 0)

    local(ng // 2, ng)
    each_chip(run)


def solution(mesh):
    spec = P(('dp', 'cy', 'cx'))

    def local(q, k, v):
        t, nh, hd = q.shape
        ng = k.shape[1]
        rep = nh // ng
        c = t // 2
        qt = q.transpose(1, 0, 2)
        any_spec = pl.BlockSpec(memory_space=pl.ANY)
        dma = pltpu.SemaphoreType.DMA
        o = pl.pallas_call(
            functools.partial(kernel, ng=ng, rep=rep, c=c, hd=hd),
            out_shape=pltpu.VMEM((nh, t, hd), jnp.bfloat16),
            in_specs=[any_spec] * 3,
            out_specs=pl.BlockSpec(memory_space=pltpu.VMEM),
            scratch_shapes=[
                pltpu.VMEM((nh, t, hd), jnp.bfloat16),
                pltpu.VMEM((t * ng, hd), jnp.bfloat16),
                pltpu.VMEM((t * ng, hd), jnp.bfloat16),
                pltpu.VMEM((2, t * ng, hd), jnp.float32),
                pltpu.VMEM((ng, 2, TILES, 2, c, hd), jnp.bfloat16),
                pltpu.VMEM((ng, 2, rep * c, 2 * c), jnp.float32),
                pltpu.VMEM((ng, 2, rep * c, 2 * c), jnp.float32),
                pltpu.VMEM((ng, 2, rep * c, hd), jnp.float32),
                dma((3,)), dma((3,)), dma((2,)), dma((2,)),
                dma((1,)), dma((ng, 3)), dma((ng,)), dma((ng, 2)),
                pltpu.SemaphoreType.REGULAR((3,)),
            ],
            compiler_params=pltpu.CompilerParams(collective_id=0, has_side_effects=True),
        )(qt, k.reshape(t * ng, hd), v.reshape(t * ng, hd))
        return o.transpose(1, 0, 2)

    return jax.shard_map(local, mesh=mesh, in_specs=(spec, spec, spec), out_specs=spec, check_vma=False)
```

time: 18.7 us -> 17.3 us (0.925)
  Pallas kernels: 17.6 us -> 16.1 us
    pallas_call x1, Pallas kernels: 17.6 us -> 16.1 us  [local(): pl.pallas_call(functools.partial(kernel, ng=ng, rep=rep, c=c, hd=hd), out...]
where the time goes in v5:
time: 17.3 us; the launch traced here: 17 us
  Pallas kernels  16.1 us (93%)
  local copies, waits for them, and re-layouts  0.93 us (5%)
    pallas_call x1, Pallas kernels, local(): pl.pallas_call(functools.partial(kernel, ng=ng, rep=rep, c=c, hd=hd), out...  16.1 us
    unnamed x1, local copies, waits for them, and re-layouts  0.93 us

profile of v5, /device:TPU:0, one launch (start us, length us, event | category | flops | bytes accessed | tf_op | source)
XLA Modules:
  0.0 17.0 jit_solution(17714149193025378306)
XLA Ops:
  0.0 16.1 %shard_map.37 = bf16[28,128,128]{2,1,0:T(8,128)(2,1)S(1)} custom-call(bf16[28,128,128]{2,1,0:T(8,128)(2,1)} %bitcast.5, bf16[512,128]{1,0:T(8,128)(2,1)} %bitcast.6, bf16[512,128]{1,0:T(8,128)(2,1)} %bitcast.7), custom_call_target="tpu_custom_call" | custom-call | tf_op jit(solution)/shard_map/pallas_call | solution.py:355
  16.1 0.9 %copy.5 = bf16[128,28,128]{2,0,1:T(8,128)(2,1)} copy(bf16[128,28,128]{2,0,1:T(8,128)(2,1)S(1)} %bitcast.4) | data formatting | bytes 1835008

commit v6 on v5

--- a/solution.py
+++ b/solution.py
@@ -29,7 +29,7 @@
 
 
 def kernel(q_hbm, k_hbm, v_hbm, out_ref, qs, kin, vin, kf, g_ref, m_ref, l_ref, acc_ref,
-           in_sem, own_send, rel_send, fwd_send, sib_recv, msg_recv, rel_recv, fwd_recv, here, *, ng, rep, c, hd):
+           in_sem, own_send, rel_send, fwd_send, sib_recv, msg_recv, rel_recv, fwd_recv, extra_recv, here, *, ng, rep, c, hd):
     icy = lax.axis_index('cy')
     icx = lax.axis_index('cx')
     core = icx % 2
@@ -51,8 +51,8 @@
     def tiles(g, run, lane):
         return g_ref.at[g, :, pl.ds(run[0], run[1]), lane]
 
-    def copy(g, src, dst, lane, send, recv, dev):
-        return remote(tiles(g, src, 0), tiles(g, dst, lane), send, recv, dev)
+    def copy(g, src, dst, lane, send, recv, dev, src_lane=0):
+        return remote(tiles(g, src, src_lane), tiles(g, dst, lane), send, recv, dev)
 
     def arrival(g, run, lane, recv):
         remote(tiles(g, run, lane), tiles(g, run, lane), own_send.at[0], recv, sdev).wait_recv()
@@ -89,7 +89,9 @@
     for t, src in enumerate((kin, vin)):
         loads[t].wait()
         kf[t] = src[...].astype(jnp.float32)
-        for g in range(ng):
+
+    def own_rows(g):
+        for t in range(2):
             x = kf[t, pl.ds(g, 2 * c, stride=ng), :].astype(jnp.bfloat16)
             g_ref[g, t, F0, 0] = x[:c]
             g_ref[g, t, S0, 0] = x[c:]
@@ -191,23 +193,27 @@
     def forward(g, run_, send, recv):
         copy(g, run_, run_, 1, send, recv, sdev).start()
 
-    def send_own(way, chip):
-        late_first = chip == 3 and way == X
-        count = len(own_list(way, chip))
-        for i in (reversed(range(count)) if late_first else range(count)):
-            for g in heads:
-                own_copy(way, chip, g, i).start()
+    def send_own(way, chip, i=0):
+        for g in heads:
+            own_copy(way, chip, g, i).start()
 
     def start_sends(chip):
         back, on = (None, X, Y, None)[chip], (None, Y, X, None)[chip]
         if back is not None:
             signal(here.at[back], devs[back])
-            send_own(back, chip)
         elif chip == 3:
             signal(here.at[X], xdev)
             signal(here.at[Y], ydev)
-            send_own(Y, chip)
-            send_own(X, chip)
+        for g in heads:
+            own_rows(g)
+            if back is not None:
+                own_copy(back, chip, g, 0).start()
+            elif chip == 3:
+                own_copy(Y, chip, g, 0).start()
+                own_copy(X, chip, g, 1).start()
+        if chip == 3:
+            send_own(Y, chip, 1)
+            send_own(X, chip, 0)
         if chip:
             @pl.when(core == 0)
             def _():
@@ -222,30 +228,69 @@
             pl.semaphore_wait(here.at[on], 1)
             send_own(on, chip)
 
+    def on_core(k, *fns):
+        @pl.when(core == k)
+        def _():
+            for f in fns:
+                f()
+
+    part = functools.partial
+
     def run(chip):
+        back = (None, X, Y, None)[chip]
+        last = ng - 1
+
+        def relay(g, way, lane=0):
+            src, dst = rel_run(way, chip, g)
+            copy(g, src, dst, lane, rel_send.at[way], rel_recv.at[g], devs[way], lane).start()
+
         def take(g, group):
             r = GROUP_RUN[chip][group]
+            by_core_1 = back is not None and group == 0 and g == last
             arrival(g, r, 0, msg_recv.at[g, group])
             for way in (X, Y):
                 rel = rel_run(way, chip, g)
                 if rel is not None and r[0] <= rel[0][0] and rel[0][0] + rel[0][1] <= r[0] + r[1]:
-                    copy(g, rel[0], rel[1], 0, rel_send.at[way], rel_recv.at[g], devs[way]).start()
+                    if by_core_1:
+                        on_core(1, functools.partial(relay, g, way))
+                    else:
+                        relay(g, way)
             stage = 1 if group == LATE else 0
-            forward(g, r, fwd_send.at[stage], fwd_recv.at[g, stage])
+            forward(g, r, fwd_send.at[stage], extra_recv.at[0] if by_core_1 else fwd_recv.at[g, stage])
+
+        def other_last():
+            arrival(last, GROUP_RUN[chip][0], 1, extra_recv.at[0])
+
+        def relay_other_last():
+            other_last()
+            relay(last, back, 1)
 
         def relayed(g):
+            if chip == 0 and g == last:
+                both = g_ref.at[g, :, pl.ds(*RELAYED[chip])]
+                remote(both, both, fwd_send.at[1], rel_recv.at[g], sdev).wait_recv()
+                remote(both, both, fwd_send.at[1], fwd_recv.at[g, 1], sdev).start()
+                return
             arrival(g, RELAYED[chip], 0, rel_recv.at[g])
             forward(g, RELAYED[chip], fwd_send.at[1], fwd_recv.at[g, 1])
 
+        def relayed_on():
+            both = g_ref.at[last, :, pl.ds(*RELAYED[chip])]
+            remote(both, both, fwd_send.at[1], fwd_recv.at[last, 1], sdev).wait_recv()
+
         def near(g):
-            arrival(g, (0, NEAR_UNITS[chip]), 1, fwd_recv.at[g, 0])
+            units = NEAR_UNITS[chip] - (1 if back is not None and g == last else 0)
+            arrival(g, (0, units), 1, fwd_recv.at[g, 0])
             attend(0, g, NEAR[0][chip], False, not FAR[0][chip])
             attend(1, g, NEAR[1][chip], False, False)
 
-        def far(g):
-            arrival(g, (0, FAR_UNITS[chip]), 1, fwd_recv.at[g, 1])
-            attend(0, g, FAR[0][chip], False, True)
-            attend(1, g, FAR[1][chip], False, True)
+        def far(*gs):
+            for g in gs:
+                if not (chip == 0 and g == last):
+                    arrival(g, (0, FAR_UNITS[chip]), 1, fwd_recv.at[g, 1])
+            for g in gs:
+                attend(0, g, FAR[0][chip], False, True)
+                attend(1, g, FAR[1][chip], False, True)
 
         def finish_own(g):
             o = acc_ref[g, 0] * (1.0 / jnp.sum(l_ref[g, 0], axis=-1, keepdims=True))
@@ -257,18 +302,13 @@
                 sent(ng, sum(d[1] for _, d in own_list(way, chip)), own_send.at[way])
                 rel = [rel_run(way, chip, g) for g in heads]
                 units = sum(r[0][1] for r in rel if r is not None)
-                if units:
-                    count = 2 if units % ng else ng
-                    sent(count, units // count, rel_send.at[way])
+                if way == back:
+                    on_core(0, part(sent, 1, units - 1, rel_send.at[way]))
+                    on_core(1, part(sent, 1, units + 1, rel_send.at[way]))
+                elif units:
+                    sent(1, units, rel_send.at[way])
             sent(ng, NEAR_UNITS[chip], fwd_send.at[0])
 
-        def on_core(k, *fns):
-            @pl.when(core == k)
-            def _():
-                for f in fns:
-                    f()
-
-        part = functools.partial
         if chip == 0:
             for g in heads:
                 finish_own(g)
@@ -277,18 +317,18 @@
                 take(g, 0)
                 near(g - 1)
             on_core(0, part(relayed, 0))
-            on_core(1, part(relayed, 0), part(relayed, 1))
+            on_core(1, part(relayed, 0), part(relayed, 1), part(relayed, 2))
             near(3)
             on_core(0, part(relayed, 1))
-            on_core(1, part(relayed, 2))
             far(0)
+            on_core(0, part(relayed, 2))
             on_core(1, part(relayed, 3))
             far(1)
             wait_sends()
-            on_core(0, part(relayed, 2))
-            far(2)
-            on_core(0, part(relayed, 3))
-            far(3)
+            on_core(0, relayed_on)
+            far(2, 3)
+            on_core(0, part(sent, 3, 2, fwd_send.at[1]))
+            on_core(1, part(sent, 2, 5, fwd_send.at[1]))
         elif chip == 3:
             take(0, 0)
             for g in range(1, ng):
@@ -301,15 +341,18 @@
                 far(g - 1)
             wait_sends()
             far(3)
+            sent(ng, FAR_UNITS[chip], fwd_send.at[1])
         else:
             for g, group in ((0, 0), (1, 0), (0, 1), (2, 0), (1, 1), (3, 0)):
                 take(g, group)
             near(0)
             take(2, 1), take(3, 1)
             near(1)
+            on_core(1, relay_other_last)
             take(0, LATE), take(1, LATE)
             near(2)
             take(2, LATE), relayed(0)
+            on_core(0, other_last)
             near(3)
             take(3, LATE), relayed(1)
             far(0)
@@ -319,7 +362,7 @@
             relayed(3)
             far(2)
             far(3)
-        sent(ng, FAR_UNITS[chip], fwd_send.at[1])
+            sent(ng, FAR_UNITS[chip], fwd_send.at[1])
 
     def each_chip(f):
         for chip in range(4):
@@ -367,7 +410,7 @@
                 pltpu.VMEM((ng, 2, rep * c, 2 * c), jnp.float32),
                 pltpu.VMEM((ng, 2, rep * c, hd), jnp.float32),
                 dma((3,)), dma((3,)), dma((2,)), dma((2,)),
-                dma((1,)), dma((ng, 3)), dma((ng,)), dma((ng, 2)),
+                dma((1,)), dma((ng, 3)), dma((ng,)), dma((ng, 2)), dma((1,)),
                 pltpu.SemaphoreType.REGULAR((3,)),
             ],
             compiler_params=pltpu.CompilerParams(collective_id=0, has_side_effects=True),

time: 17.3 us -> 17.1 us (0.988)
  no operation moved by 1% of the time
where the time goes in v6:
time: 17.1 us; the launch traced here: 17 us
  Pallas kernels  16.1 us (94%)
  local copies, waits for them, and re-layouts  0.93 us (5%)
    pallas_call x1, Pallas kernels, local(): pl.pallas_call(functools.partial(kernel, ng=ng, rep=rep, c=c, hd=hd), out...  16.1 us
    unnamed x1, local copies, waits for them, and re-layouts  0.93 us

profile of v6, /device:TPU:0, one launch (start us, length us, event | category | flops | bytes accessed | tf_op | source)
XLA Modules:
  0.0 17.0 jit_solution(13718130361034316421)
XLA Ops:
  0.0 16.1 %shard_map.37 = bf16[28,128,128]{2,1,0:T(8,128)(2,1)S(1)} custom-call(bf16[28,128,128]{2,1,0:T(8,128)(2,1)} %bitcast.5, bf16[512,128]{1,0:T(8,128)(2,1)} %bitcast.6, bf16[512,128]{1,0:T(8,128)(2,1)} %bitcast.7), custom_call_target="tpu_custom_call" | custom-call | tf_op jit(solution)/shard_map/pallas_call | solution.py:398
  16.1 0.9 %copy.5 = bf16[128,28,128]{2,0,1:T(8,128)(2,1)} copy(bf16[128,28,128]{2,0,1:T(8,128)(2,1)S(1)} %bitcast.4) | data formatting | bytes 1835008

commit v7 on v6

--- a/solution.py
+++ b/solution.py
@@ -312,23 +312,20 @@
         if chip == 0:
             for g in heads:
                 finish_own(g)
-            take(0, 0)
-            for g in range(1, ng):
-                take(g, 0)
-                near(g - 1)
-            on_core(0, part(relayed, 0))
-            on_core(1, part(relayed, 0), part(relayed, 1), part(relayed, 2))
+            on_core(0, part(take, 0, 0))
+            on_core(1, part(take, 0, 0), part(take, 1, 0), part(take, 2, 0))
+            near(0)
+            on_core(0, part(take, 1, 0))
+            on_core(1, part(take, 3, 0))
+            near(1)
+            on_core(0, part(take, 2, 0))
+            near(2)
+            on_core(0, part(take, 3, 0))
+            on_core(1, *[part(relayed, g) for g in heads])
             near(3)
-            on_core(0, part(relayed, 1))
-            far(0)
-            on_core(0, part(relayed, 2))
-            on_core(1, part(relayed, 3))
-            far(1)
-            wait_sends()
-            on_core(0, relayed_on)
-            far(2, 3)
-            on_core(0, part(sent, 3, 2, fwd_send.at[1]))
-            on_core(1, part(sent, 2, 5, fwd_send.at[1]))
+            on_core(0, part(relayed, 0), part(far, 0), part(relayed, 1), part(far, 1), part(relayed, 2), part(far, 2),
+                    wait_sends, relayed_on, part(far, 3), part(sent, 3, 2, fwd_send.at[1]))
+            on_core(1, part(far, 0, 1), wait_sends, part(far, 2, 3), part(sent, 2, 5, fwd_send.at[1]))
         elif chip == 3:
             take(0, 0)
             for g in range(1, ng):

time: 17.1 us -> 16.6 us (0.971)
  Pallas kernels: 16.1 us -> 15.4 us
    pallas_call x1, Pallas kernels: 16.1 us -> 15.4 us  [local(): pl.pallas_call(functools.partial(kernel, ng=ng, rep=rep, c=c, hd=hd), out...]
where the time goes in v7:
time: 16.6 us; the launch traced here: 16.4 us
  Pallas kernels  15.4 us (93%)
  local copies, waits for them, and re-layouts  0.93 us (6%)
    pallas_call x1, Pallas kernels, local(): pl.pallas_call(functools.partial(kernel, ng=ng, rep=rep, c=c, hd=hd), out...  15.4 us
    unnamed x1, local copies, waits for them, and re-layouts  0.93 us

profile of v7, /device:TPU:0, one launch (start us, length us, event | category | flops | bytes accessed | tf_op | source)
XLA Modules:
  0.0 16.4 jit_solution(3206698595400621545)
XLA Ops:
  0.0 15.4 %shard_map.37 = bf16[28,128,128]{2,1,0:T(8,128)(2,1)S(1)} custom-call(bf16[28,128,128]{2,1,0:T(8,128)(2,1)} %bitcast.5, bf16[512,128]{1,0:T(8,128)(2,1)} %bitcast.6, bf16[512,128]{1,0:T(8,128)(2,1)} %bitcast.7), custom_call_target="tpu_custom_call" | custom-call | tf_op jit(solution)/shard_map/pallas_call | solution.py:395
  15.5 0.9 %copy.5 = bf16[128,28,128]{2,0,1:T(8,128)(2,1)} copy(bf16[128,28,128]{2,0,1:T(8,128)(2,1)S(1)} %bitcast.4) | data formatting | bytes 1835008

commit v8 on v7

--- a/solution.py
+++ b/solution.py
@@ -26,10 +26,12 @@
 NEAR_UNITS = (4, 2, 2, 2)
 FAR_UNITS = (2, 3, 2, 1)
 RELAYED = ((F3, 2), (F3, 2), (F3, 1), (F3, 1))
+BY_CHIP_3 = (0, 3)
+BY_CORE_1 = (2, 3)
 
 
 def kernel(q_hbm, k_hbm, v_hbm, out_ref, qs, kin, vin, kf, g_ref, m_ref, l_ref, acc_ref,
-           in_sem, own_send, rel_send, fwd_send, sib_recv, msg_recv, rel_recv, fwd_recv, extra_recv, here, *, ng, rep, c, hd):
+           in_sem, send, sib_recv, msg_recv, rel_recv, fwd_recv, extra_recv, here, *, ng, rep, c, hd):
     icy = lax.axis_index('cy')
     icx = lax.axis_index('cx')
     core = icx % 2
@@ -44,22 +46,27 @@
     def signal(sem, dev):
         pl.semaphore_signal(sem, inc=1, device_id=dev, device_id_type=MESH)
 
-    def remote(src, dst, send, recv, dev):
-        return pltpu.make_async_remote_copy(src_ref=src, dst_ref=dst, send_sem=send, recv_sem=recv,
+    def remote(src, dst, snd, recv, dev):
+        return pltpu.make_async_remote_copy(src_ref=src, dst_ref=dst, send_sem=snd, recv_sem=recv,
                                             device_id=dev, device_id_type=MESH)
 
     def tiles(g, run, lane):
         return g_ref.at[g, :, pl.ds(run[0], run[1]), lane]
 
-    def copy(g, src, dst, lane, send, recv, dev, src_lane=0):
-        return remote(tiles(g, src, src_lane), tiles(g, dst, lane), send, recv, dev)
+    def copy(g, src, dst, lane, snd, recv, dev, src_lane=0):
+        return remote(tiles(g, src, src_lane), tiles(g, dst, lane), snd, recv, dev)
 
     def arrival(g, run, lane, recv):
-        remote(tiles(g, run, lane), tiles(g, run, lane), own_send.at[0], recv, sdev).wait_recv()
-
-    def sent(count, units, send):
-        ref = g_ref.at[pl.ds(0, count), :, pl.ds(0, units), 0]
-        remote(ref, ref, send, sib_recv.at[0], sdev).wait_send()
+        remote(tiles(g, run, lane), tiles(g, run, lane), send.at[0], recv, sdev).wait_recv()
+
+    def sent(units, i):
+        for count in (4, 3, 2, 1):
+            if units % count == 0 and units // count <= 2 * TILES:
+                break
+        n = units // count
+        lanes = 1 if n <= TILES else 2
+        ref = g_ref.at[pl.ds(0, count), :, pl.ds(0, n // lanes), pl.ds(0, lanes)]
+        remote(ref, ref, send.at[i], sib_recv.at[0], sdev).wait_send()
 
     loads = [
         pltpu.make_async_copy(k_hbm, kin, in_sem.at[0]),
@@ -175,23 +182,23 @@
     def own_copy(way, frm, g, i):
         to = frm ^ (1, 2)[way]
         src, dst = own_list(way, frm)[i]
-        return copy(g, src, dst, 0, own_send.at[way], msg_recv.at[g, GROUP[to][way][i]], devs[way])
+        return copy(g, src, dst, 0, send.at[0], msg_recv.at[g, GROUP[to][way][i]], devs[way])
 
     def rel_run(way, frm, g):
         if way == Y:
             if frm == 2:
                 return (S1, 1), (S3, 1)
-            if frm == 3 and g >= 2:
+            if frm == 3 and g not in BY_CHIP_3:
                 return None
             return (F1, 1), (F3, 1)
         if frm == 0:
-            return ((S2, 1), (S3, 1)) if g < 2 else ((F2, 2), (F3, 2))
+            return ((S2, 1), (S3, 1)) if g in BY_CHIP_3 else ((F2, 2), (F3, 2))
         if frm == 1:
             return (F2, 1), (F3, 1)
         return None
 
-    def forward(g, run_, send, recv):
-        copy(g, run_, run_, 1, send, recv, sdev).start()
+    def forward(g, run_, snd, recv):
+        copy(g, run_, run_, 1, snd, recv, sdev).start()
 
     def send_own(way, chip, i=0):
         for g in heads:
@@ -200,10 +207,10 @@
     def start_sends(chip):
         back, on = (None, X, Y, None)[chip], (None, Y, X, None)[chip]
         if back is not None:
-            signal(here.at[back], devs[back])
+            signal(here.at[0], devs[back])
         elif chip == 3:
-            signal(here.at[X], xdev)
-            signal(here.at[Y], ydev)
+            signal(here.at[0], xdev)
+            signal(here.at[0], ydev)
         for g in heads:
             own_rows(g)
             if back is not None:
@@ -217,15 +224,15 @@
         if chip:
             @pl.when(core == 0)
             def _():
-                signal(here.at[SIB], sdev)
+                signal(here.at[1], sdev)
 
             @pl.when(core == 1)
             def _():
-                pl.semaphore_wait(here.at[SIB], 1)
+                pl.semaphore_wait(here.at[1], 1)
         for g in heads:
-            copy(g, (S0, 2), (S0, 2), 1, own_send.at[SIB], sib_recv.at[0], sdev).start()
+            copy(g, (S0, 2), (S0, 2), 1, send.at[0], sib_recv.at[0], sdev).start()
         if on is not None:
-            pl.semaphore_wait(here.at[on], 1)
+            pl.semaphore_wait(here.at[0], 1)
             send_own(on, chip)
 
     def on_core(k, *fns):
@@ -238,55 +245,58 @@
 
     def run(chip):
         back = (None, X, Y, None)[chip]
-        last = ng - 1
 
         def relay(g, way, lane=0):
             src, dst = rel_run(way, chip, g)
-            copy(g, src, dst, lane, rel_send.at[way], rel_recv.at[g], devs[way], lane).start()
+            copy(g, src, dst, lane, send.at[1], rel_recv.at[g], devs[way], lane).start()
 
         def take(g, group):
             r = GROUP_RUN[chip][group]
-            by_core_1 = back is not None and group == 0 and g == last
+            by_core_1 = back is not None and group == 0 and g in BY_CORE_1
             arrival(g, r, 0, msg_recv.at[g, group])
             for way in (X, Y):
                 rel = rel_run(way, chip, g)
                 if rel is not None and r[0] <= rel[0][0] and rel[0][0] + rel[0][1] <= r[0] + r[1]:
                     if by_core_1:
-                        on_core(1, functools.partial(relay, g, way))
+                        if g != BY_CORE_1[-1]:
+                            on_core(1, part(relay, g, way))
                     else:
                         relay(g, way)
             stage = 1 if group == LATE else 0
-            forward(g, r, fwd_send.at[stage], extra_recv.at[0] if by_core_1 else fwd_recv.at[g, stage])
-
-        def other_last():
-            arrival(last, GROUP_RUN[chip][0], 1, extra_recv.at[0])
-
-        def relay_other_last():
-            other_last()
-            relay(last, back, 1)
+            recv = extra_recv.at[BY_CORE_1.index(g)] if by_core_1 else fwd_recv.at[g, stage]
+            forward(g, r, send.at[2 * stage], recv)
+
+        def other(g):
+            arrival(g, GROUP_RUN[chip][0], 1, extra_recv.at[BY_CORE_1.index(g)])
+
+        def relay_other(g):
+            other(g)
+            relay(g, back, 1)
+
+        def both_lanes(g):
+            ref = g_ref.at[g, :, pl.ds(*RELAYED[chip])]
+            return (lambda recv: remote(ref, ref, send.at[2], recv, sdev))
 
         def relayed(g):
-            if chip == 0 and g == last:
-                both = g_ref.at[g, :, pl.ds(*RELAYED[chip])]
-                remote(both, both, fwd_send.at[1], rel_recv.at[g], sdev).wait_recv()
-                remote(both, both, fwd_send.at[1], fwd_recv.at[g, 1], sdev).start()
+            if chip == 0 and g in BY_CORE_1:
+                both_lanes(g)(rel_recv.at[g]).wait_recv()
+                both_lanes(g)(fwd_recv.at[g, 1]).start()
                 return
             arrival(g, RELAYED[chip], 0, rel_recv.at[g])
-            forward(g, RELAYED[chip], fwd_send.at[1], fwd_recv.at[g, 1])
-
-        def relayed_on():
-            both = g_ref.at[last, :, pl.ds(*RELAYED[chip])]
-            remote(both, both, fwd_send.at[1], fwd_recv.at[last, 1], sdev).wait_recv()
+            forward(g, RELAYED[chip], send.at[2], fwd_recv.at[g, 1])
+
+        def relayed_on(g):
+            both_lanes(g)(fwd_recv.at[g, 1]).wait_recv()
 
         def near(g):
-            units = NEAR_UNITS[chip] - (1 if back is not None and g == last else 0)
+            units = NEAR_UNITS[chip] - (1 if back is not None and g in BY_CORE_1 else 0)
             arrival(g, (0, units), 1, fwd_recv.at[g, 0])
             attend(0, g, NEAR[0][chip], False, not FAR[0][chip])
             attend(1, g, NEAR[1][chip], False, False)
 
         def far(*gs):
             for g in gs:
-                if not (chip == 0 and g == last):
+                if not (chip == 0 and g in BY_CORE_1):
                     arrival(g, (0, FAR_UNITS[chip]), 1, fwd_recv.at[g, 1])
             for g in gs:
                 attend(0, g, FAR[0][chip], False, True)
@@ -297,17 +307,17 @@
             out_ref[rep * g:rep * (g + 1), :c, :] = o.astype(jnp.bfloat16).reshape(rep, c, hd)
 
         def wait_sends():
-            sent(ng, 2, own_send.at[SIB])
-            for way in (X, Y):
-                sent(ng, sum(d[1] for _, d in own_list(way, chip)), own_send.at[way])
-                rel = [rel_run(way, chip, g) for g in heads]
-                units = sum(r[0][1] for r in rel if r is not None)
-                if way == back:
-                    on_core(0, part(sent, 1, units - 1, rel_send.at[way]))
-                    on_core(1, part(sent, 1, units + 1, rel_send.at[way]))
-                elif units:
-                    sent(1, units, rel_send.at[way])
-            sent(ng, NEAR_UNITS[chip], fwd_send.at[0])
+            own = 2 + sum(d[1] for way in (X, Y) for _, d in own_list(way, chip))
+            sent(ng * (own + NEAR_UNITS[chip]), 0)
+            rel = [rel_run(way, chip, g) for way in (X, Y) for g in heads]
+            units = sum(r[0][1] for r in rel if r is not None)
+            if back is not None:
+                on_core(0, part(sent, units - len(BY_CORE_1), 1))
+                on_core(1, part(sent, units + len(BY_CORE_1), 1))
+            else:
+                sent(units, 1)
+
+        far_sent = part(sent, ng * FAR_UNITS[chip], 2)
 
         if chip == 0:
             for g in heads:
@@ -319,13 +329,14 @@
             on_core(1, part(take, 3, 0))
             near(1)
             on_core(0, part(take, 2, 0))
+            on_core(1, part(relayed, 0), part(relayed, 1))
             near(2)
             on_core(0, part(take, 3, 0))
-            on_core(1, *[part(relayed, g) for g in heads])
+            on_core(1, part(relayed, 2))
             near(3)
-            on_core(0, part(relayed, 0), part(far, 0), part(relayed, 1), part(far, 1), part(relayed, 2), part(far, 2),
-                    wait_sends, relayed_on, part(far, 3), part(sent, 3, 2, fwd_send.at[1]))
-            on_core(1, part(far, 0, 1), wait_sends, part(far, 2, 3), part(sent, 2, 5, fwd_send.at[1]))
+            on_core(0, part(relayed, 0), part(far, 0), part(relayed, 1), part(far, 1), wait_sends,
+                    part(relayed_on, 2), part(far, 2), part(relayed_on, 3), part(far, 3), part(sent, 4, 2))
+            on_core(1, part(relayed, 3), part(far, 2, 3), wait_sends, part(far, 0, 1), part(sent, 12, 2))
         elif chip == 3:
             take(0, 0)
             for g in range(1, ng):
@@ -338,18 +349,20 @@
                 far(g - 1)
             wait_sends()
             far(3)
-            sent(ng, FAR_UNITS[chip], fwd_send.at[1])
+            far_sent()
         else:
             for g, group in ((0, 0), (1, 0), (0, 1), (2, 0), (1, 1), (3, 0)):
                 take(g, group)
             near(0)
             take(2, 1), take(3, 1)
+            on_core(1, part(relay_other, 2), part(relay, 3, back))
             near(1)
-            on_core(1, relay_other_last)
+            on_core(1, part(relay_other, 3))
             take(0, LATE), take(1, LATE)
+            on_core(0, part(other, 2))
             near(2)
             take(2, LATE), relayed(0)
-            on_core(0, other_last)
+            on_core(0, part(other, 3))
             near(3)
             take(3, LATE), relayed(1)
             far(0)
@@ -359,7 +372,7 @@
             relayed(3)
             far(2)
             far(3)
-            sent(ng, FAR_UNITS[chip], fwd_send.at[1])
+            far_sent()
 
     def each_chip(f):
         for chip in range(4):
@@ -368,14 +381,14 @@
     each_chip(start_sends)
     loads[2].wait()
     own = g_ref.at[:, :, pl.ds(S0, 2), 1]
-    remote(own, own, own_send.at[SIB], sib_recv.at[0], sdev).wait_recv()
+    remote(own, own, send.at[0], sib_recv.at[0], sdev).wait_recv()
     local(0, ng // 2)
 
     @pl.when(chip_index == 0)
     def _():
-        for way in (X, Y):
-            pl.semaphore_wait(here.at[way], 1)
-            send_own(way, 0)
+        pl.semaphore_wait(here.at[0], 2)
+        send_own(X, 0)
+        send_own(Y, 0)
 
     local(ng // 2, ng)
     each_chip(run)
@@ -406,9 +419,9 @@
                 pltpu.VMEM((ng, 2, rep * c, 2 * c), jnp.float32),
                 pltpu.VMEM((ng, 2, rep * c, 2 * c), jnp.float32),
                 pltpu.VMEM((ng, 2, rep * c, hd), jnp.float32),
-                dma((3,)), dma((3,)), dma((2,)), dma((2,)),
-                dma((1,)), dma((ng, 3)), dma((ng,)), dma((ng, 2)), dma((1,)),
-                pltpu.SemaphoreType.REGULAR((3,)),
+                dma((3,)), dma((3,)),
+                dma((1,)), dma((ng, 3)), dma((ng,)), dma((ng, 2)), dma((2,)),
+                pltpu.SemaphoreType.REGULAR((2,)),
             ],
             compiler_params=pltpu.CompilerParams(collective_id=0, has_side_effects=True),
         )(qt, k.reshape(t * ng, hd), v.reshape(t * ng, hd))

time: 16.6 us -> 16.5 us (level)
  no operation moved by 1% of the time
where the time goes in v8:
time: 16.5 us; the launch traced here: 16.4 us
  Pallas kernels  15.4 us (93%)
  local copies, waits for them, and re-layouts  0.93 us (6%)
    pallas_call x1, Pallas kernels, local(): pl.pallas_call(functools.partial(kernel, ng=ng, rep=rep, c=c, hd=hd), out...  15.4 us
    unnamed x1, local copies, waits for them, and re-layouts  0.93 us

profile of v8, /device:TPU:0, one launch (start us, length us, event | category | flops | bytes accessed | tf_op | source)
XLA Modules:
  0.0 16.4 jit_solution(18118183572548798309)
XLA Ops:
  0.0 15.4 %shard_map.37 = bf16[28,128,128]{2,1,0:T(8,128)(2,1)S(1)} custom-call(bf16[28,128,128]{2,1,0:T(8,128)(2,1)} %bitcast.5, bf16[512,128]{1,0:T(8,128)(2,1)} %bitcast.6, bf16[512,128]{1,0:T(8,128)(2,1)} %bitcast.7), custom_call_target="tpu_custom_call" | custom-call | tf_op jit(solution)/shard_map/pallas_call | solution.py:408
  15.4 0.9 %copy.5 = bf16[128,28,128]{2,0,1:T(8,128)(2,1)} copy(bf16[128,28,128]{2,0,1:T(8,128)(2,1)S(1)} %bitcast.4) | data formatting | bytes 1835008

commit v9 on v8

--- a/solution.py
+++ b/solution.py
@@ -73,8 +73,8 @@
         pltpu.make_async_copy(v_hbm, vin, in_sem.at[1]),
         pltpu.make_async_copy(q_hbm, qs, in_sem.at[2]),
     ]
-    for cp in loads:
-        cp.start()
+    loads[0].start()
+    loads[1].start()
 
     @pl.when(chip_index == 0)
     def _():
@@ -95,6 +95,8 @@
 
     for t, src in enumerate((kin, vin)):
         loads[t].wait()
+        if t:
+            loads[2].start()
         kf[t] = src[...].astype(jnp.float32)
 
     def own_rows(g):
@@ -182,7 +184,9 @@
     def own_copy(way, frm, g, i):
         to = frm ^ (1, 2)[way]
         src, dst = own_list(way, frm)[i]
-        return copy(g, src, dst, 0, send.at[0], msg_recv.at[g, GROUP[to][way][i]], devs[way])
+        group = GROUP[to][way][i]
+        recv = rel_recv.at[g] if group == LATE else msg_recv.at[g, group]
+        return copy(g, src, dst, 0, send.at[0], recv, devs[way])
 
     def rel_run(way, frm, g):
         if way == Y:
@@ -248,7 +252,8 @@
 
         def relay(g, way, lane=0):
             src, dst = rel_run(way, chip, g)
-            copy(g, src, dst, lane, send.at[1], rel_recv.at[g], devs[way], lane).start()
+            recv = extra_recv.at[1] if lane and g == BY_CORE_1[-1] else rel_recv.at[g]
+            copy(g, src, dst, lane, send.at[1], recv, devs[way], lane).start()
 
         def take(g, group):
             r = GROUP_RUN[chip][group]
@@ -262,9 +267,8 @@
                             on_core(1, part(relay, g, way))
                     else:
                         relay(g, way)
-            stage = 1 if group == LATE else 0
-            recv = extra_recv.at[BY_CORE_1.index(g)] if by_core_1 else fwd_recv.at[g, stage]
-            forward(g, r, send.at[2 * stage], recv)
+            recv = extra_recv.at[BY_CORE_1.index(g)] if by_core_1 else fwd_recv.at[g, 0]
+            forward(g, r, send.at[0], recv)
 
         def other(g):
             arrival(g, GROUP_RUN[chip][0], 1, extra_recv.at[BY_CORE_1.index(g)])
@@ -273,20 +277,32 @@
             other(g)
             relay(g, back, 1)
 
+        def lanes(g, lane, count):
+            ref = g_ref.at[g, :, pl.ds(*RELAYED[chip]), pl.ds(lane, count)]
+            return lambda recv: remote(ref, ref, send.at[2], recv, sdev)
+
         def both_lanes(g):
-            ref = g_ref.at[g, :, pl.ds(*RELAYED[chip])]
-            return (lambda recv: remote(ref, ref, send.at[2], recv, sdev))
+            if g != BY_CORE_1[-1]:
+                return ((lanes(g, 0, 2), rel_recv.at[g], fwd_recv.at[g, 1]),)
+            return ((lanes(g, 0, 1), rel_recv.at[g], fwd_recv.at[g, 1]),
+                    (lanes(g, 1, 1), extra_recv.at[1], extra_recv.at[1]))
 
         def relayed(g):
             if chip == 0 and g in BY_CORE_1:
-                both_lanes(g)(rel_recv.at[g]).wait_recv()
-                both_lanes(g)(fwd_recv.at[g, 1]).start()
+                for cp, recv, on in both_lanes(g):
+                    cp(recv).wait_recv()
+                    cp(on).start()
                 return
-            arrival(g, RELAYED[chip], 0, rel_recv.at[g])
+            if back is None:
+                arrival(g, RELAYED[chip], 0, rel_recv.at[g])
+            else:
+                arrival(g, (0, FAR_UNITS[chip]), 0, rel_recv.at[g])
+                forward(g, GROUP_RUN[chip][LATE], send.at[2], fwd_recv.at[g, 1])
             forward(g, RELAYED[chip], send.at[2], fwd_recv.at[g, 1])
 
         def relayed_on(g):
-            both_lanes(g)(fwd_recv.at[g, 1]).wait_recv()
+            for cp, _, on in both_lanes(g):
+                cp(on).wait_recv()
 
         def near(g):
             units = NEAR_UNITS[chip] - (1 if back is not None and g in BY_CORE_1 else 0)
@@ -334,9 +350,9 @@
             on_core(0, part(take, 3, 0))
             on_core(1, part(relayed, 2))
             near(3)
+            on_core(1, part(relayed, 3), part(far, 2, 3), wait_sends, part(far, 0, 1), part(sent, 12, 2))
             on_core(0, part(relayed, 0), part(far, 0), part(relayed, 1), part(far, 1), wait_sends,
                     part(relayed_on, 2), part(far, 2), part(relayed_on, 3), part(far, 3), part(sent, 4, 2))
-            on_core(1, part(relayed, 3), part(far, 2, 3), wait_sends, part(far, 0, 1), part(sent, 12, 2))
         elif chip == 3:
             take(0, 0)
             for g in range(1, ng):
@@ -358,13 +374,12 @@
             on_core(1, part(relay_other, 2), part(relay, 3, back))
             near(1)
             on_core(1, part(relay_other, 3))
-            take(0, LATE), take(1, LATE)
             on_core(0, part(other, 2))
             near(2)
-            take(2, LATE), relayed(0)
+            relayed(0)
             on_core(0, part(other, 3))
             near(3)
-            take(3, LATE), relayed(1)
+            relayed(1)
             far(0)
             relayed(2)
             far(1)
@@ -375,7 +390,7 @@
             far_sent()
 
     def each_chip(f):
-        for chip in range(4):
+        for chip in (3, 2, 1, 0):
             pl.when(chip_index == chip)(functools.partial(f, chip))
 
     each_chip(start_sends)
@@ -420,7 +435,7 @@
                 pltpu.VMEM((ng, 2, rep * c, 2 * c), jnp.float32),
                 pltpu.VMEM((ng, 2, rep * c, hd), jnp.float32),
                 dma((3,)), dma((3,)),
-                dma((1,)), dma((ng, 3)), dma((ng,)), dma((ng, 2)), dma((2,)),
+                dma((1,)), dma((ng, 2)), dma((ng,)), dma((ng, 2)), dma((2,)),
                 pltpu.SemaphoreType.REGULAR((2,)),
             ],
             compiler_params=pltpu.CompilerParams(collective_id=0, has_side_effects=True),

time: 16.5 us -> 16.3 us (0.988)
  Pallas kernels: 15.4 us -> 15.2 us
    pallas_call x1, Pallas kernels: 15.4 us -> 15.2 us  [local(): pl.pallas_call(functools.partial(kernel, ng=ng, rep=rep, c=c, hd=hd), out...]
where the time goes in v9:
time: 16.3 us; the launch traced here: 16.2 us
  Pallas kernels  15.2 us (93%)
  local copies, waits for them, and re-layouts  0.93 us (6%)
    pallas_call x1, Pallas kernels, local(): pl.pallas_call(functools.partial(kernel, ng=ng, rep=rep, c=c, hd=hd), out...  15.2 us
    unnamed x1, local copies, waits for them, and re-layouts  0.93 us

profile of v9, /device:TPU:0, one launch (start us, length us, event | category | flops | bytes accessed | tf_op | source)
XLA Modules:
  0.0 16.2 jit_solution(3166206416671410751)
XLA Ops:
  0.0 15.2 %shard_map.37 = bf16[28,128,128]{2,1,0:T(8,128)(2,1)S(1)} custom-call(bf16[28,128,128]{2,1,0:T(8,128)(2,1)} %bitcast.5, bf16[512,128]{1,0:T(8,128)(2,1)} %bitcast.6, bf16[512,128]{1,0:T(8,128)(2,1)} %bitcast.7), custom_call_target="tpu_custom_call" | custom-call | tf_op jit(solution)/shard_map/pallas_call | solution.py:423
  15.2 0.9 %copy.5 = bf16[128,28,128]{2,0,1:T(8,128)(2,1)} copy(bf16[128,28,128]{2,0,1:T(8,128)(2,1)S(1)} %bitcast.4) | data formatting | bytes 1835008

commit v10 on v9

--- a/solution.py
+++ b/solution.py
@@ -28,6 +28,7 @@
 RELAYED = ((F3, 2), (F3, 2), (F3, 1), (F3, 1))
 BY_CHIP_3 = (0, 3)
 BY_CORE_1 = (2, 3)
+LAST = 3
 
 
 def kernel(q_hbm, k_hbm, v_hbm, out_ref, qs, kin, vin, kf, g_ref, m_ref, l_ref, acc_ref,
@@ -192,12 +193,12 @@
         if way == Y:
             if frm == 2:
                 return (S1, 1), (S3, 1)
-            if frm == 3 and g not in BY_CHIP_3:
+            if frm == 3 and g not in BY_CHIP_3 or frm == 0 and g == LAST:
                 return None
             return (F1, 1), (F3, 1)
         if frm == 0:
             return ((S2, 1), (S3, 1)) if g in BY_CHIP_3 else ((F2, 2), (F3, 2))
-        if frm == 1:
+        if frm == 1 or frm == 3 and g == LAST:
             return (F2, 1), (F3, 1)
         return None
 
@@ -252,8 +253,10 @@
 
         def relay(g, way, lane=0):
             src, dst = rel_run(way, chip, g)
-            recv = extra_recv.at[1] if lane and g == BY_CORE_1[-1] else rel_recv.at[g]
-            copy(g, src, dst, lane, send.at[1], recv, devs[way], lane).start()
+            dev = devs[way]
+            if way == back and g == LAST:
+                dev = {'cy': icy, 'cx': (icx + 2) % 4 - 1} if way == X else {'cy': (icy + 1) % 2, 'cx': icx - 1}
+            copy(g, src, dst, lane, send.at[1], rel_recv.at[g], dev, lane).start()
 
         def take(g, group):
             r = GROUP_RUN[chip][group]
@@ -263,7 +266,7 @@
                 rel = rel_run(way, chip, g)
                 if rel is not None and r[0] <= rel[0][0] and rel[0][0] + rel[0][1] <= r[0] + r[1]:
                     if by_core_1:
-                        if g != BY_CORE_1[-1]:
+                        if g != LAST:
                             on_core(1, part(relay, g, way))
                     else:
                         relay(g, way)
@@ -277,21 +280,14 @@
             other(g)
             relay(g, back, 1)
 
-        def lanes(g, lane, count):
-            ref = g_ref.at[g, :, pl.ds(*RELAYED[chip]), pl.ds(lane, count)]
-            return lambda recv: remote(ref, ref, send.at[2], recv, sdev)
-
-        def both_lanes(g):
-            if g != BY_CORE_1[-1]:
-                return ((lanes(g, 0, 2), rel_recv.at[g], fwd_recv.at[g, 1]),)
-            return ((lanes(g, 0, 1), rel_recv.at[g], fwd_recv.at[g, 1]),
-                    (lanes(g, 1, 1), extra_recv.at[1], extra_recv.at[1]))
+        def both_lanes(g, recv):
+            ref = g_ref.at[g, :, pl.ds(*RELAYED[chip])]
+            return remote(ref, ref, send.at[2], recv, sdev)
 
         def relayed(g):
             if chip == 0 and g in BY_CORE_1:
-                for cp, recv, on in both_lanes(g):
-                    cp(recv).wait_recv()
-                    cp(on).start()
+                both_lanes(g, rel_recv.at[g]).wait_recv()
+                both_lanes(g, fwd_recv.at[g, 1]).start()
                 return
             if back is None:
                 arrival(g, RELAYED[chip], 0, rel_recv.at[g])
@@ -301,8 +297,7 @@
             forward(g, RELAYED[chip], send.at[2], fwd_recv.at[g, 1])
 
         def relayed_on(g):
-            for cp, _, on in both_lanes(g):
-                cp(on).wait_recv()
+            both_lanes(g, fwd_recv.at[g, 1]).wait_recv()
 
         def near(g):
             units = NEAR_UNITS[chip] - (1 if back is not None and g in BY_CORE_1 else 0)
@@ -350,9 +345,9 @@
             on_core(0, part(take, 3, 0))
             on_core(1, part(relayed, 2))
             near(3)
-            on_core(1, part(relayed, 3), part(far, 2, 3), wait_sends, part(far, 0, 1), part(sent, 12, 2))
+            on_core(1, part(far, 2), part(far, 0, 1), wait_sends, part(relayed_on, 3), part(far, 3), part(sent, 8, 2))
             on_core(0, part(relayed, 0), part(far, 0), part(relayed, 1), part(far, 1), wait_sends,
-                    part(relayed_on, 2), part(far, 2), part(relayed_on, 3), part(far, 3), part(sent, 4, 2))
+                    part(relayed_on, 2), part(relayed, 3), part(far, 2, 3), part(sent, 8, 2))
         elif chip == 3:
             take(0, 0)
             for g in range(1, ng):

time: 16.3 us -> 16 us (0.982)
  Pallas kernels: 15.2 us -> 15 us
    pallas_call x1, Pallas kernels: 15.2 us -> 15 us  [local(): pl.pallas_call(functools.partial(kernel, ng=ng, rep=rep, c=c, hd=hd), out...]
where the time goes in v10:
time: 16 us; the launch traced here: 15.9 us
  Pallas kernels  15 us (94%)
  local copies, waits for them, and re-layouts  0.93 us (6%)
    pallas_call x1, Pallas kernels, local(): pl.pallas_call(functools.partial(kernel, ng=ng, rep=rep, c=c, hd=hd), out...  15 us
    unnamed x1, local copies, waits for them, and re-layouts  0.93 us

profile of v10, /device:TPU:0, one launch (start us, length us, event | category | flops | bytes accessed | tf_op | source)
XLA Modules:
  0.0 15.9 jit_solution(14890045171948106558)
XLA Ops:
  0.0 15.0 %shard_map.37 = bf16[28,128,128]{2,1,0:T(8,128)(2,1)S(1)} custom-call(bf16[28,128,128]{2,1,0:T(8,128)(2,1)} %bitcast.5, bf16[512,128]{1,0:T(8,128)(2,1)} %bitcast.6, bf16[512,128]{1,0:T(8,128)(2,1)} %bitcast.7), custom_call_target="tpu_custom_call" | custom-call | tf_op jit(solution)/shard_map/pallas_call | solution.py:418
  15.0 0.9 %copy.5 = bf16[128,28,128]{2,0,1:T(8,128)(2,1)} copy(bf16[128,28,128]{2,0,1:T(8,128)(2,1)S(1)} %bitcast.4) | data formatting | bytes 1835008

commit v11 on v10

--- a/solution.py
+++ b/solution.py
@@ -15,13 +15,13 @@
 TILES = 9
 X, Y, SIB = 0, 1, 2
 
-NEAR = (((), ((F1, 1),), ((F2, 1),), ((F1, 2),)),
-        (((S1, 4),), ((F1, 2),), ((S1, 1), (F2, 1)), ((F1, 2),)))
+NEAR = (((), ((F1, 1),), ((F1, 1),), ((F1, 2),)),
+        (((S1, 4),), ((F1, 2),), ((S1, 2),), ((F1, 2),)))
 FAR = (((), (), ((F3, 1),), ((F3, 1),)),
-       (((F3, 2),), ((S2, 1), (F3, 2)), ((F1, 1), (F3, 1)), ((F3, 1),)))
+       (((F3, 2),), ((S2, 1), (F3, 2)), ((F3, 2),), ((F3, 1),)))
 
 GROUP = (((0,), (0,)), ((1,), (0, 2)), ((2, 0), (1,)), ((0,), (0,)))
-GROUP_RUN = (((S1, 4),), ((F2, 1), (F1, 1), (S2, 1)), ((S1, 1), (F2, 1), (F1, 1)), ((F1, 2),))
+GROUP_RUN = (((S1, 4),), ((F2, 1), (F1, 1), (S2, 1)), ((S1, 1), (F1, 1), (S3, 1)), ((F1, 2),))
 LATE = 2
 NEAR_UNITS = (4, 2, 2, 2)
 FAR_UNITS = (2, 3, 2, 1)
@@ -175,8 +175,9 @@
     heads = range(ng)
 
     def own_list(way, frm):
-        f = (F0, 1), ((F1, 1), (F2, 1))[way]
-        if frm ^ (1, 2)[way] > frm:
+        to = frm ^ (1, 2)[way]
+        f = (F0, 1), (((S3, 1), (F1, 1)) if to == 2 else ((F1, 1), (F2, 1)))[way]
+        if to > frm:
             return [f]
         if frm == 3:
             return [f, ((S0, 1), ((S1, 1), (S2, 1))[way])]
@@ -256,7 +257,8 @@
             dev = devs[way]
             if way == back and g == LAST:
                 dev = {'cy': icy, 'cx': (icx + 2) % 4 - 1} if way == X else {'cy': (icy + 1) % 2, 'cx': icx - 1}
-            copy(g, src, dst, lane, send.at[1], rel_recv.at[g], dev, lane).start()
+            recv = extra_recv.at[1] if lane and g == LAST else rel_recv.at[g]
+            copy(g, src, dst, lane, send.at[1], recv, dev, lane).start()
 
         def take(g, group):
             r = GROUP_RUN[chip][group]
@@ -280,14 +282,20 @@
             other(g)
             relay(g, back, 1)
 
-        def both_lanes(g, recv):
-            ref = g_ref.at[g, :, pl.ds(*RELAYED[chip])]
-            return remote(ref, ref, send.at[2], recv, sdev)
+        def lanes(g):
+            def part_of(lane, count, recv, on):
+                ref = g_ref.at[g, :, pl.ds(*RELAYED[chip]), pl.ds(lane, count)]
+                return remote(ref, ref, send.at[2], recv, sdev), remote(ref, ref, send.at[2], on, sdev)
+
+            if g != LAST:
+                return (part_of(0, 2, rel_recv.at[g], fwd_recv.at[g, 1]),)
+            return (part_of(0, 1, rel_recv.at[g], fwd_recv.at[g, 1]), part_of(1, 1, extra_recv.at[1], extra_recv.at[1]))
 
         def relayed(g):
             if chip == 0 and g in BY_CORE_1:
-                both_lanes(g, rel_recv.at[g]).wait_recv()
-                both_lanes(g, fwd_recv.at[g, 1]).start()
+                for come, go in lanes(g):
+                    come.wait_recv()
+                    go.start()
                 return
             if back is None:
                 arrival(g, RELAYED[chip], 0, rel_recv.at[g])
@@ -297,7 +305,8 @@
             forward(g, RELAYED[chip], send.at[2], fwd_recv.at[g, 1])
 
         def relayed_on(g):
-            both_lanes(g, fwd_recv.at[g, 1]).wait_recv()
+            for _, go in lanes(g):
+                go.wait_recv()
 
         def near(g):
             units = NEAR_UNITS[chip] - (1 if back is not None and g in BY_CORE_1 else 0)
@@ -347,7 +356,7 @@
             near(3)
             on_core(1, part(far, 2), part(far, 0, 1), wait_sends, part(relayed_on, 3), part(far, 3), part(sent, 8, 2))
             on_core(0, part(relayed, 0), part(far, 0), part(relayed, 1), part(far, 1), wait_sends,
-                    part(relayed_on, 2), part(relayed, 3), part(far, 2, 3), part(sent, 8, 2))
+                    part(relayed, 3), part(relayed_on, 2), part(far, 2, 3), part(sent, 8, 2))
         elif chip == 3:
             take(0, 0)
             for g in range(1, ng):

time: 16 us -> 15.8 us (0.988)
  Pallas kernels: 15 us -> 14.7 us
    pallas_call x1, Pallas kernels: 15 us -> 14.7 us  [local(): pl.pallas_call(functools.partial(kernel, ng=ng, rep=rep, c=c, hd=hd), out...]
where the time goes in v11:
time: 15.8 us; the launch traced here: 15.6 us
  Pallas kernels  14.7 us (93%)
  local copies, waits for them, and re-layouts  0.93 us (6%)
    pallas_call x1, Pallas kernels, local(): pl.pallas_call(functools.partial(kernel, ng=ng, rep=rep, c=c, hd=hd), out...  14.7 us
    unnamed x1, local copies, waits for them, and re-layouts  0.93 us

profile of v11, /device:TPU:0, one launch (start us, length us, event | category | flops | bytes accessed | tf_op | source)
XLA Modules:
  0.0 15.6 jit_solution(6759919508641140238)
XLA Ops:
  0.0 14.7 %shard_map.37 = bf16[28,128,128]{2,1,0:T(8,128)(2,1)S(1)} custom-call(bf16[28,128,128]{2,1,0:T(8,128)(2,1)} %bitcast.5, bf16[512,128]{1,0:T(8,128)(2,1)} %bitcast.6, bf16[512,128]{1,0:T(8,128)(2,1)} %bitcast.7), custom_call_target="tpu_custom_call" | custom-call | tf_op jit(solution)/shard_map/pallas_call | solution.py:427
  14.7 0.9 %copy.5 = bf16[128,28,128]{2,0,1:T(8,128)(2,1)} copy(bf16[128,28,128]{2,0,1:T(8,128)(2,1)S(1)} %bitcast.4) | data formatting | bytes 1835008

commit v12 on v11

--- a/solution.py
+++ b/solution.py
@@ -61,12 +61,14 @@
         remote(tiles(g, run, lane), tiles(g, run, lane), send.at[0], recv, sdev).wait_recv()
 
     def sent(units, i):
-        for count in (4, 3, 2, 1):
-            if units % count == 0 and units // count <= 2 * TILES:
-                break
-        n = units // count
-        lanes = 1 if n <= TILES else 2
-        ref = g_ref.at[pl.ds(0, count), :, pl.ds(0, n // lanes), pl.ds(0, lanes)]
+        fits = [(count, units // count) for count in (4, 3, 2, 1) if units % count == 0]
+        fits = [(count, n) for count, n in fits if n <= TILES or n % 2 == 0 and n <= 2 * TILES]
+        if fits:
+            count, n = fits[0]
+            lanes = 1 if n <= TILES else 2
+            ref = g_ref.at[pl.ds(0, count), :, pl.ds(0, n // lanes), pl.ds(0, lanes)]
+        else:
+            ref = kf.at[:, pl.ds(0, units * c // 2)]
         remote(ref, ref, send.at[i], sib_recv.at[0], sdev).wait_send()
 
     loads = [
@@ -74,8 +76,11 @@
         pltpu.make_async_copy(v_hbm, vin, in_sem.at[1]),
         pltpu.make_async_copy(q_hbm, qs, in_sem.at[2]),
     ]
-    loads[0].start()
-    loads[1].start()
+    rows = kin.shape[0] // 4
+    for i in range(4):
+        for t, (hbm, vmem) in enumerate(((k_hbm, kin), (v_hbm, vin))):
+            piece = pl.ds(i * rows, rows)
+            pltpu.make_async_copy(hbm.at[piece], vmem.at[piece], in_sem.at[t]).start()
 
     @pl.when(chip_index == 0)
     def _():
@@ -255,10 +260,20 @@
         def relay(g, way, lane=0):
             src, dst = rel_run(way, chip, g)
             dev = devs[way]
-            if way == back and g == LAST:
-                dev = {'cy': icy, 'cx': (icx + 2) % 4 - 1} if way == X else {'cy': (icy + 1) % 2, 'cx': icx - 1}
-            recv = extra_recv.at[1] if lane and g == LAST else rel_recv.at[g]
+            recv = rel_recv.at[g]
+            if way == back and g in BY_CORE_1:
+                if g == LAST:
+                    if lane:
+                        core_0 = to_core_0(way)
+                        copy(g, src, dst, lane, send.at[1], extra_recv.at[1], core_0, lane).start()
+                    else:
+                        dev = to_core_0(way)
+                elif lane:
+                    recv = extra_recv.at[0]
             copy(g, src, dst, lane, send.at[1], recv, dev, lane).start()
+
+        def to_core_0(way):
+            return {'cy': icy, 'cx': (icx + 2) % 4 - 1} if way == X else {'cy': (icy + 1) % 2, 'cx': icx - 1}
 
         def take(g, group):
             r = GROUP_RUN[chip][group]
@@ -282,31 +297,24 @@
             other(g)
             relay(g, back, 1)
 
-        def lanes(g):
-            def part_of(lane, count, recv, on):
-                ref = g_ref.at[g, :, pl.ds(*RELAYED[chip]), pl.ds(lane, count)]
-                return remote(ref, ref, send.at[2], recv, sdev), remote(ref, ref, send.at[2], on, sdev)
-
-            if g != LAST:
-                return (part_of(0, 2, rel_recv.at[g], fwd_recv.at[g, 1]),)
-            return (part_of(0, 1, rel_recv.at[g], fwd_recv.at[g, 1]), part_of(1, 1, extra_recv.at[1], extra_recv.at[1]))
+        def lane_copy(g, lane, recv):
+            ref = tiles(g, RELAYED[chip], lane)
+            return remote(ref, ref, send.at[2], recv, sdev)
+
+        def lane_in(g, lane, recv):
+            lane_copy(g, lane, recv).wait_recv()
+
+        def lane_on(g, lane, recv, on):
+            lane_in(g, lane, recv)
+            lane_copy(g, lane, on).start()
 
         def relayed(g):
-            if chip == 0 and g in BY_CORE_1:
-                for come, go in lanes(g):
-                    come.wait_recv()
-                    go.start()
-                return
             if back is None:
                 arrival(g, RELAYED[chip], 0, rel_recv.at[g])
             else:
                 arrival(g, (0, FAR_UNITS[chip]), 0, rel_recv.at[g])
                 forward(g, GROUP_RUN[chip][LATE], send.at[2], fwd_recv.at[g, 1])
             forward(g, RELAYED[chip], send.at[2], fwd_recv.at[g, 1])
-
-        def relayed_on(g):
-            for _, go in lanes(g):
-                go.wait_recv()
 
         def near(g):
             units = NEAR_UNITS[chip] - (1 if back is not None and g in BY_CORE_1 else 0)
@@ -333,7 +341,7 @@
             units = sum(r[0][1] for r in rel if r is not None)
             if back is not None:
                 on_core(0, part(sent, units - len(BY_CORE_1), 1))
-                on_core(1, part(sent, units + len(BY_CORE_1), 1))
+                on_core(1, part(sent, units + len(BY_CORE_1) + 1, 1))
             else:
                 sent(units, 1)
 
@@ -352,11 +360,15 @@
             on_core(1, part(relayed, 0), part(relayed, 1))
             near(2)
             on_core(0, part(take, 3, 0))
-            on_core(1, part(relayed, 2))
+            on_core(1, part(lane_on, 2, 0, rel_recv.at[2], fwd_recv.at[2, 1]),
+                    part(lane_on, 2, 1, extra_recv.at[0], extra_recv.at[0]))
             near(3)
-            on_core(1, part(far, 2), part(far, 0, 1), wait_sends, part(relayed_on, 3), part(far, 3), part(sent, 8, 2))
-            on_core(0, part(relayed, 0), part(far, 0), part(relayed, 1), part(far, 1), wait_sends,
-                    part(relayed, 3), part(relayed_on, 2), part(far, 2, 3), part(sent, 8, 2))
+            on_core(1, part(far, 2, 0), wait_sends, part(lane_in, 3, 1, rel_recv.at[3]),
+                    part(lane_in, 3, 0, fwd_recv.at[3, 1]), part(far, 1, 3), part(sent, 8, 2))
+            on_core(0, part(relayed, 0), part(far, 0), part(relayed, 1),
+                    part(lane_on, 3, 0, rel_recv.at[3], fwd_recv.at[3, 1]), part(far, 1), wait_sends,
+                    part(lane_in, 2, 0, fwd_recv.at[2, 1]), part(lane_in, 2, 1, extra_recv.at[0]),
+                    part(lane_in, 3, 1, extra_recv.at[1]), part(far, 2, 3), part(sent, 6, 2))
         elif chip == 3:
             take(0, 0)
             for g in range(1, ng):

time: 15.8 us -> 15.6 us (0.987)
  Pallas kernels: 14.7 us -> 14.4 us
    pallas_call x1, Pallas kernels: 14.7 us -> 14.4 us  [local(): pl.pallas_call(functools.partial(kernel, ng=ng, rep=rep, c=c, hd=hd), out...]
where the time goes in v12:
time: 15.6 us; the launch traced here: 15.3 us
  Pallas kernels  14.4 us (92%)
  local copies, waits for them, and re-layouts  0.93 us (6%)
    pallas_call x1, Pallas kernels, local(): pl.pallas_call(functools.partial(kernel, ng=ng, rep=rep, c=c, hd=hd), out...  14.4 us
    unnamed x1, local copies, waits for them, and re-layouts  0.93 us

profile of v12, /device:TPU:0, one launch (start us, length us, event | category | flops | bytes accessed | tf_op | source)
XLA Modules:
  0.0 15.3 jit_solution(10552585459777764576)
XLA Ops:
  0.0 14.4 %shard_map.37 = bf16[28,128,128]{2,1,0:T(8,128)(2,1)S(1)} custom-call(bf16[28,128,128]{2,1,0:T(8,128)(2,1)} %bitcast.5, bf16[512,128]{1,0:T(8,128)(2,1)} %bitcast.6, bf16[512,128]{1,0:T(8,128)(2,1)} %bitcast.7), custom_call_target="tpu_custom_call" | custom-call | tf_op jit(solution)/shard_map/pallas_call | solution.py:439
  14.4 0.9 %copy.5 = bf16[128,28,128]{2,0,1:T(8,128)(2,1)} copy(bf16[128,28,128]{2,0,1:T(8,128)(2,1)S(1)} %bitcast.4) | data formatting | bytes 1835008

commit v13 on v12

--- a/solution.py
+++ b/solution.py
@@ -71,16 +71,12 @@
             ref = kf.at[:, pl.ds(0, units * c // 2)]
         remote(ref, ref, send.at[i], sib_recv.at[0], sdev).wait_send()
 
-    loads = [
-        pltpu.make_async_copy(k_hbm, kin, in_sem.at[0]),
-        pltpu.make_async_copy(v_hbm, vin, in_sem.at[1]),
-        pltpu.make_async_copy(q_hbm, qs, in_sem.at[2]),
-    ]
-    rows = kin.shape[0] // 4
-    for i in range(4):
-        for t, (hbm, vmem) in enumerate(((k_hbm, kin), (v_hbm, vin))):
+    load_q = pltpu.make_async_copy(q_hbm, qs, in_sem.at[0])
+    rows = kin.shape[0] // 8
+    for i in range(8):
+        for hbm, vmem in ((k_hbm, kin), (v_hbm, vin)):
             piece = pl.ds(i * rows, rows)
-            pltpu.make_async_copy(hbm.at[piece], vmem.at[piece], in_sem.at[t]).start()
+            pltpu.make_async_copy(hbm.at[piece], vmem.at[piece], in_sem.at[0]).start()
 
     @pl.when(chip_index == 0)
     def _():
@@ -99,10 +95,10 @@
     def _():
         signal(barrier, sdev)
 
+    both = 2 * kin.shape[0] // qs.shape[1]
+    pltpu.make_async_copy(q_hbm.at[pl.ds(0, both)], qs.at[pl.ds(0, both)], in_sem.at[0]).wait()
+    load_q.start()
     for t, src in enumerate((kin, vin)):
-        loads[t].wait()
-        if t:
-            loads[2].start()
         kf[t] = src[...].astype(jnp.float32)
 
     def own_rows(g):
@@ -192,7 +188,7 @@
         to = frm ^ (1, 2)[way]
         src, dst = own_list(way, frm)[i]
         group = GROUP[to][way][i]
-        recv = rel_recv.at[g] if group == LATE else msg_recv.at[g, group]
+        recv = (msg_recv.at[g], msg_recv.at[ng + g // 2], rel_recv.at[g])[group]
         return copy(g, src, dst, 0, send.at[0], recv, devs[way])
 
     def rel_run(way, frm, g):
@@ -278,7 +274,11 @@
         def take(g, group):
             r = GROUP_RUN[chip][group]
             by_core_1 = back is not None and group == 0 and g in BY_CORE_1
-            arrival(g, r, 0, msg_recv.at[g, group])
+            if group == 0:
+                arrival(g, r, 0, msg_recv.at[g])
+            elif g % 2 == 0:
+                pair = g_ref.at[pl.ds(g, 2), :, pl.ds(*r), 0]
+                remote(pair, pair, send.at[0], msg_recv.at[ng + g // 2], sdev).wait_recv()
             for way in (X, Y):
                 rel = rel_run(way, chip, g)
                 if rel is not None and r[0] <= rel[0][0] and rel[0][0] + rel[0][1] <= r[0] + r[1]:
@@ -383,7 +383,7 @@
             far(3)
             far_sent()
         else:
-            for g, group in ((0, 0), (1, 0), (0, 1), (2, 0), (1, 1), (3, 0)):
+            for g, group in ((0, 0), (1, 0), (2, 0), (0, 1), (1, 1), (3, 0)):
                 take(g, group)
             near(0)
             take(2, 1), take(3, 1)
@@ -410,7 +410,7 @@
             pl.when(chip_index == chip)(functools.partial(f, chip))
 
     each_chip(start_sends)
-    loads[2].wait()
+    load_q.wait()
     own = g_ref.at[:, :, pl.ds(S0, 2), 1]
     remote(own, own, send.at[0], sib_recv.at[0], sdev).wait_recv()
     local(0, ng // 2)
@@ -450,8 +450,8 @@
                 pltpu.VMEM((ng, 2, rep * c, 2 * c), jnp.float32),
                 pltpu.VMEM((ng, 2, rep * c, 2 * c), jnp.float32),
                 pltpu.VMEM((ng, 2, rep * c, hd), jnp.float32),
-                dma((3,)), dma((3,)),
-                dma((1,)), dma((ng, 2)), dma((ng,)), dma((ng, 2)), dma((2,)),
+                dma((1,)), dma((3,)),
+                dma((1,)), dma((ng + ng // 2,)), dma((ng,)), dma((ng, 2)), dma((2,)),
                 pltpu.SemaphoreType.REGULAR((2,)),
             ],
             compiler_params=pltpu.CompilerParams(collective_id=0, has_side_effects=True),

time: 15.6 us -> 15.6 us (level)
  no operation moved by 1% of the time
where the time goes in v13:
time: 15.6 us; the launch traced here: 15.4 us
  Pallas kernels  14.4 us (92%)
  local copies, waits for them, and re-layouts  0.93 us (6%)
    pallas_call x1, Pallas kernels, local(): pl.pallas_call(functools.partial(kernel, ng=ng, rep=rep, c=c, hd=hd), out...  14.4 us
    unnamed x1, local copies, waits for them, and re-layouts  0.93 us

profile of v13, /device:TPU:0, one launch (start us, length us, event | category | flops | bytes accessed | tf_op | source)
XLA Modules:
  0.0 15.4 jit_solution(3768690692988880624)
XLA Ops:
  0.0 14.4 %shard_map.37 = bf16[28,128,128]{2,1,0:T(8,128)(2,1)S(1)} custom-call(bf16[28,128,128]{2,1,0:T(8,128)(2,1)} %bitcast.5, bf16[512,128]{1,0:T(8,128)(2,1)} %bitcast.6, bf16[512,128]{1,0:T(8,128)(2,1)} %bitcast.7), custom_call_target="tpu_custom_call" | custom-call | tf_op jit(solution)/shard_map/pallas_call | solution.py:439
  14.4 0.9 %copy.5 = bf16[128,28,128]{2,0,1:T(8,128)(2,1)} copy(bf16[128,28,128]{2,0,1:T(8,128)(2,1)S(1)} %bitcast.4) | data formatting | bytes 1835008

commit v14 on v13

--- a/solution.py
+++ b/solution.py
@@ -72,11 +72,11 @@
         remote(ref, ref, send.at[i], sib_recv.at[0], sdev).wait_send()
 
     load_q = pltpu.make_async_copy(q_hbm, qs, in_sem.at[0])
-    rows = kin.shape[0] // 8
-    for i in range(8):
-        for hbm, vmem in ((k_hbm, kin), (v_hbm, vin)):
+    rows = kin.shape[0] // 4
+    for t, (hbm, vmem) in enumerate(((k_hbm, kin), (v_hbm, vin))):
+        for i in range(4):
             piece = pl.ds(i * rows, rows)
-            pltpu.make_async_copy(hbm.at[piece], vmem.at[piece], in_sem.at[0]).start()
+            pltpu.make_async_copy(hbm.at[piece], vmem.at[piece], in_sem.at[t]).start()
 
     @pl.when(chip_index == 0)
     def _():
@@ -95,10 +95,10 @@
     def _():
         signal(barrier, sdev)
 
-    both = 2 * kin.shape[0] // qs.shape[1]
-    pltpu.make_async_copy(q_hbm.at[pl.ds(0, both)], qs.at[pl.ds(0, both)], in_sem.at[0]).wait()
-    load_q.start()
-    for t, src in enumerate((kin, vin)):
+    for t, (hbm, src) in enumerate(((k_hbm, kin), (v_hbm, vin))):
+        pltpu.make_async_copy(hbm, src, in_sem.at[t]).wait()
+        if t:
+            load_q.start()
         kf[t] = src[...].astype(jnp.float32)
 
     def own_rows(g):
@@ -450,7 +450,7 @@
                 pltpu.VMEM((ng, 2, rep * c, 2 * c), jnp.float32),
                 pltpu.VMEM((ng, 2, rep * c, 2 * c), jnp.float32),
                 pltpu.VMEM((ng, 2, rep * c, hd), jnp.float32),
-                dma((1,)), dma((3,)),
+                dma((2,)), dma((3,)),
                 dma((1,)), dma((ng + ng // 2,)), dma((ng,)), dma((ng, 2)), dma((2,)),
                 pltpu.SemaphoreType.REGULAR((2,)),
             ],

time: 15.6 us -> 15.5 us (level)
  no operation moved by 1% of the time
where the time goes in v14:
time: 15.5 us; the launch traced here: 15.3 us
  Pallas kernels  14.4 us (93%)
  local copies, waits for them, and re-layouts  0.93 us (6%)
    pallas_call x1, Pallas kernels, local(): pl.pallas_call(functools.partial(kernel, ng=ng, rep=rep, c=c, hd=hd), out...  14.4 us
    unnamed x1, local copies, waits for them, and re-layouts  0.93 us

profile of v14, /device:TPU:0, one launch (start us, length us, event | category | flops | bytes accessed | tf_op | source)
XLA Modules:
  0.0 15.3 jit_solution(12722168154886834767)
XLA Ops:
  0.0 14.4 %shard_map.37 = bf16[28,128,128]{2,1,0:T(8,128)(2,1)S(1)} custom-call(bf16[28,128,128]{2,1,0:T(8,128)(2,1)} %bitcast.5, bf16[512,128]{1,0:T(8,128)(2,1)} %bitcast.6, bf16[512,128]{1,0:T(8,128)(2,1)} %bitcast.7), custom_call_target="tpu_custom_call" | custom-call | tf_op jit(solution)/shard_map/pallas_call | solution.py:439
  14.4 0.9 %copy.5 = bf16[128,28,128]{2,0,1:T(8,128)(2,1)} copy(bf16[128,28,128]{2,0,1:T(8,128)(2,1)S(1)} %bitcast.4) | data formatting | bytes 1835008

commit v15 on v14

--- a/solution.py
+++ b/solution.py
@@ -72,9 +72,9 @@
         remote(ref, ref, send.at[i], sib_recv.at[0], sdev).wait_send()
 
     load_q = pltpu.make_async_copy(q_hbm, qs, in_sem.at[0])
-    rows = kin.shape[0] // 4
+    rows = kin.shape[0] // 8
     for t, (hbm, vmem) in enumerate(((k_hbm, kin), (v_hbm, vin))):
-        for i in range(4):
+        for i in range(8):
             piece = pl.ds(i * rows, rows)
             pltpu.make_async_copy(hbm.at[piece], vmem.at[piece], in_sem.at[t]).start()
 

time: 15.5 us -> 15.6 us (level)
  no operation moved by 1% of the time
where the time goes in v15:
time: 15.6 us; the launch traced here: 15.4 us
  Pallas kernels  14.4 us (92%)
  local copies, waits for them, and re-layouts  0.93 us (6%)
    pallas_call x1, Pallas kernels, local(): pl.pallas_call(functools.partial(kernel, ng=ng, rep=rep, c=c, hd=hd), out...  14.4 us
    unnamed x1, local copies, waits for them, and re-layouts  0.93 us

profile of v15, /device:TPU:0, one launch (start us, length us, event | category | flops | bytes accessed | tf_op | source)
XLA Modules:
  0.0 15.4 jit_solution(9909300791962658327)
XLA Ops:
  0.0 14.4 %shard_map.37 = bf16[28,128,128]{2,1,0:T(8,128)(2,1)S(1)} custom-call(bf16[28,128,128]{2,1,0:T(8,128)(2,1)} %bitcast.5, bf16[512,128]{1,0:T(8,128)(2,1)} %bitcast.6, bf16[512,128]{1,0:T(8,128)(2,1)} %bitcast.7), custom_call_target="tpu_custom_call" | custom-call | tf_op jit(solution)/shard_map/pallas_call | solution.py:439
  14.4 0.9 %copy.5 = bf16[128,28,128]{2,0,1:T(8,128)(2,1)} copy(bf16[128,28,128]{2,0,1:T(8,128)(2,1)S(1)} %bitcast.4) | data formatting | bytes 1835008

commit v16 on v15

--- a/solution.py
+++ b/solution.py
@@ -72,9 +72,9 @@
         remote(ref, ref, send.at[i], sib_recv.at[0], sdev).wait_send()
 
     load_q = pltpu.make_async_copy(q_hbm, qs, in_sem.at[0])
-    rows = kin.shape[0] // 8
+    rows = kin.shape[0] // 2
     for t, (hbm, vmem) in enumerate(((k_hbm, kin), (v_hbm, vin))):
-        for i in range(8):
+        for i in range(2):
             piece = pl.ds(i * rows, rows)
             pltpu.make_async_copy(hbm.at[piece], vmem.at[piece], in_sem.at[t]).start()
 

time: 15.6 us -> 15.6 us (level)
  no operation moved by 1% of the time
where the time goes in v16:
time: 15.6 us; the launch traced here: 15.4 us
  Pallas kernels  14.5 us (93%)
  local copies, waits for them, and re-layouts  0.93 us (6%)
    pallas_call x1, Pallas kernels, local(): pl.pallas_call(functools.partial(kernel, ng=ng, rep=rep, c=c, hd=hd), out...  14.5 us
    unnamed x1, local copies, waits for them, and re-layouts  0.93 us

profile of v16, /device:TPU:0, one launch (start us, length us, event | category | flops | bytes accessed | tf_op | source)
XLA Modules:
  0.0 15.4 jit_solution(14463331539663549851)
XLA Ops:
  0.0 14.5 %shard_map.37 = bf16[28,128,128]{2,1,0:T(8,128)(2,1)S(1)} custom-call(bf16[28,128,128]{2,1,0:T(8,128)(2,1)} %bitcast.5, bf16[512,128]{1,0:T(8,128)(2,1)} %bitcast.6, bf16[512,128]{1,0:T(8,128)(2,1)} %bitcast.7), custom_call_target="tpu_custom_call" | custom-call | tf_op jit(solution)/shard_map/pallas_call | solution.py:439
  14.5 0.9 %copy.5 = bf16[128,28,128]{2,0,1:T(8,128)(2,1)} copy(bf16[128,28,128]{2,0,1:T(8,128)(2,1)S(1)} %bitcast.4) | data formatting | bytes 1835008

commit v17 on v14

--- a/solution.py
+++ b/solution.py
@@ -365,8 +365,8 @@
             near(3)
             on_core(1, part(far, 2, 0), wait_sends, part(lane_in, 3, 1, rel_recv.at[3]),
                     part(lane_in, 3, 0, fwd_recv.at[3, 1]), part(far, 1, 3), part(sent, 8, 2))
-            on_core(0, part(relayed, 0), part(far, 0), part(relayed, 1),
-                    part(lane_on, 3, 0, rel_recv.at[3], fwd_recv.at[3, 1]), part(far, 1), wait_sends,
+            on_core(0, part(relayed, 0), part(far, 0), part(relayed, 1), wait_sends,
+                    part(lane_on, 3, 0, rel_recv.at[3], fwd_recv.at[3, 1]), part(far, 1),
                     part(lane_in, 2, 0, fwd_recv.at[2, 1]), part(lane_in, 2, 1, extra_recv.at[0]),
                     part(lane_in, 3, 1, extra_recv.at[1]), part(far, 2, 3), part(sent, 6, 2))
         elif chip == 3:

time: 15.5 us -> 15.5 us (level)
  no operation moved by 1% of the time
where the time goes in v17:
time: 15.5 us; the launch traced here: 15.3 us
  Pallas kernels  14.4 us (93%)
  local copies, waits for them, and re-layouts  0.93 us (6%)
    pallas_call x1, Pallas kernels, local(): pl.pallas_call(functools.partial(kernel, ng=ng, rep=rep, c=c, hd=hd), out...  14.4 us
    unnamed x1, local copies, waits for them, and re-layouts  0.93 us

profile of v17, /device:TPU:0, one launch (start us, length us, event | category | flops | bytes accessed | tf_op | source)
XLA Modules:
  0.0 15.3 jit_solution(8922267252057806013)
XLA Ops:
  0.0 14.4 %shard_map.37 = bf16[28,128,128]{2,1,0:T(8,128)(2,1)S(1)} custom-call(bf16[28,128,128]{2,1,0:T(8,128)(2,1)} %bitcast.5, bf16[512,128]{1,0:T(8,128)(2,1)} %bitcast.6, bf16[512,128]{1,0:T(8,128)(2,1)} %bitcast.7), custom_call_target="tpu_custom_call" | custom-call | tf_op jit(solution)/shard_map/pallas_call | solution.py:439
  14.4 0.9 %copy.5 = bf16[128,28,128]{2,0,1:T(8,128)(2,1)} copy(bf16[128,28,128]{2,0,1:T(8,128)(2,1)S(1)} %bitcast.4) | data formatting | bytes 1835008

commit v18 on v14

--- a/solution.py
+++ b/solution.py
@@ -73,8 +73,8 @@
 
     load_q = pltpu.make_async_copy(q_hbm, qs, in_sem.at[0])
     rows = kin.shape[0] // 4
-    for t, (hbm, vmem) in enumerate(((k_hbm, kin), (v_hbm, vin))):
-        for i in range(4):
+    for i in range(4):
+        for t, (hbm, vmem) in enumerate(((k_hbm, kin), (v_hbm, vin))):
             piece = pl.ds(i * rows, rows)
             pltpu.make_async_copy(hbm.at[piece], vmem.at[piece], in_sem.at[t]).start()
 

time: 15.5 us -> 15.6 us (level)
  no operation moved by 1% of the time
where the time goes in v18:
time: 15.6 us; the launch traced here: 15.3 us
  Pallas kernels  14.4 us (92%)
  local copies, waits for them, and re-layouts  0.93 us (6%)
    pallas_call x1, Pallas kernels, local(): pl.pallas_call(functools.partial(kernel, ng=ng, rep=rep, c=c, hd=hd), out...  14.4 us
    unnamed x1, local copies, waits for them, and re-layouts  0.93 us

profile of v18, /device:TPU:0, one launch (start us, length us, event | category | flops | bytes accessed | tf_op | source)
XLA Modules:
  0.0 15.3 jit_solution(8067612390230503676)
XLA Ops:
  0.0 14.4 %shard_map.37 = bf16[28,128,128]{2,1,0:T(8,128)(2,1)S(1)} custom-call(bf16[28,128,128]{2,1,0:T(8,128)(2,1)} %bitcast.5, bf16[512,128]{1,0:T(8,128)(2,1)} %bitcast.6, bf16[512,128]{1,0:T(8,128)(2,1)} %bitcast.7), custom_call_target="tpu_custom_call" | custom-call | tf_op jit(solution)/shard_map/pallas_call | solution.py:439
  14.4 0.9 %copy.5 = bf16[128,28,128]{2,0,1:T(8,128)(2,1)} copy(bf16[128,28,128]{2,0,1:T(8,128)(2,1)S(1)} %bitcast.4) | data formatting | bytes 1835008
